TPU v7x, 32 devices: a whole 2x2x4 slice. The times are simulated.
32 devices in a mesh: sector: 4 (over y, core), ops: 8 (over z, x).
Axes of the slice: x: 2, y: 2, z: 4, core: 2. Of those that a mesh axis runs over, the one named last changes fastest.
Arguments:
- wavefunction: bfloat16 [4, 1024, 1024], P('sector', 'ops'), may hold values from -6 to 6
- diag_scale: float32 [4, 1024, 1024], P('sector', 'ops'), may hold values from 1 to 8
- sector_dims: int32 [4], P('sector'), may hold values from 512 to 1024
- left_ops: bfloat16 [4, 16, 1024, 1024], P('sector', 'ops'), may hold values from -0.1875 to 0.1875
- right_ops: bfloat16 [4, 16, 1024, 1024], P('sector', 'ops'), may hold values from -0.1875 to 0.1875
- weight_index: int32 [4, 16], P('sector', 'ops'), may hold values from 0 to 15
- weight_table: float32 [16], replicated, may hold values from -1 to 1
Outputs:
- basis: bfloat16 [4, 1024, 1024], P('sector', 'ops')
- energy: float32 [4], P('sector')
- next_ops: float32 [1024, 1024], P('ops')
All inputs are finite; a program needn't handle non-finite values.
Results may differ from a plain program's by a relative error of at most 0.025.
Values may be sent and summed in bfloat16 or wider, within the bound.
A program may use at most 128 MiB of HBM per device.

v0:
```python
import functools

import jax
import jax.numpy as jnp
from jax import lax
from jax.experimental import pallas as pl
from jax.experimental.pallas import tpu as pltpu
from jax.sharding import PartitionSpec as P

BLOCK = 128
SUB = 8


def split3(u):
    high = u.astype(jnp.bfloat16).astype(jnp.float32)
    rest = u - high
    mid = rest.astype(jnp.bfloat16).astype(jnp.float32)
    low = (rest - mid).astype(jnp.bfloat16).astype(jnp.float32)
    return high, mid, low


def inverse_factor(block):
    size = block.shape[0]
    lane = lax.broadcasted_iota(jnp.int32, (SUB, size), 1)
    row = lax.broadcasted_iota(jnp.int32, (SUB, size), 0)
    below = block
    done = []
    for s in range(size // SUB):
        at = s * SUB
        top = below[:SUB]
        columns = [
            jnp.broadcast_to(top[:, at + j : at + j + 1], (SUB, size)) for j in range(SUB)
        ]
        here = (lane >= at) & (lane < at + SUB)
        body = jnp.where(here, (lane - at == row).astype(jnp.float32), top)
        pivots = jnp.ones((SUB, size), jnp.float32)
        for j in range(SUB):
            pivot = jnp.broadcast_to(columns[j][j : j + 1], (SUB, size))
            pivots = jnp.where(row == j, pivot, pivots)
            if j < SUB - 1:
                factor = jnp.where(row > j, columns[j] / pivot, 0.0)
                for c in range(j + 1, SUB):
                    columns[c] = columns[c] - factor * columns[c][j : j + 1]
                body = body - factor * body[j : j + 1]
        scaled = body * lax.rsqrt(pivots)
        done.append(scaled)
        if at + SUB < size:
            high, mid, low = split3(scaled)
            left = jnp.concatenate([high, high, mid, high, mid, low], axis=0)
            right = jnp.concatenate([high, mid, high, low, mid, high], axis=0)
            outer = lax.dot_general(
                left.T.astype(jnp.bfloat16),
                right.astype(jnp.bfloat16),
                (((1,), (0,)), ((), ())),
                preferred_element_type=jnp.float32,
            )
            rows_left = size - at - SUB
            lanes = lax.broadcasted_iota(jnp.int32, (rows_left, size), 1)
            kept = jnp.where((lanes >= at) & (lanes < at + SUB), 0.0, below[SUB:])
            below = kept - outer[at + SUB :]
    whole = jnp.concatenate(done, axis=0)
    r = lax.broadcasted_iota(jnp.int32, (size, size), 0)
    c = lax.broadcasted_iota(jnp.int32, (size, size), 1)
    return jnp.where(c <= r, whole, 0.0)


def inverse_kernel(scale, gram_ref, high_ref, low_ref, work):
    order = gram_ref.shape[0]
    blocks = order // BLOCK
    column = lax.broadcasted_iota(jnp.int32, (BLOCK, order), 1)
    local = lax.broadcasted_iota(jnp.int32, (BLOCK, order), 0)

    def rows(i):
        return pl.ds(pl.multiple_of(i * BLOCK, BLOCK), BLOCK)

    def load(i, carry):
        eye = (column == local + i * BLOCK).astype(jnp.float32)
        work[rows(i), :] = gram_ref[rows(i), :] * scale + 0.001 * eye
        return carry

    lax.fori_loop(0, blocks, load, 0)

    def step(k, carry):
        first = k * BLOCK
        inverse = inverse_factor(work[rows(k), rows(k)])
        in_k = (column >= first) & (column < first + BLOCK)
        pivot_rows = jnp.where(
            in_k, (column - first == local).astype(jnp.float32), work[rows(k), :]
        )
        work[rows(k), :] = jnp.dot(
            inverse,
            pivot_rows,
            precision=lax.Precision.HIGHEST,
            preferred_element_type=jnp.float32,
        )

        def update(i, inner):
            panel = work[rows(k), rows(i)].T
            kept = jnp.where(in_k, 0.0, work[rows(i), :])
            work[rows(i), :] = kept - jnp.dot(
                panel,
                work[rows(k), :],
                precision=lax.Precision.HIGHEST,
                preferred_element_type=jnp.float32,
            )
            return inner

        lax.fori_loop(k + 1, blocks, update, 0)
        return carry

    lax.fori_loop(0, blocks, step, 0)

    def store(i, carry):
        kept = jnp.where(column <= local + i * BLOCK, work[rows(i), :], 0.0)
        high = kept.astype(jnp.bfloat16)
        high_ref[rows(i), :] = high
        low_ref[rows(i), :] = (kept - high.astype(jnp.float32)).astype(jnp.bfloat16)
        return carry

    lax.fori_loop(0, blocks, store, 0)


def inverse_cholesky(product, scale):
    order = product.shape[0]
    half = jax.ShapeDtypeStruct((order, order), jnp.bfloat16)
    vmem = pl.BlockSpec(memory_space=pltpu.VMEM)
    return pl.pallas_call(
        functools.partial(inverse_kernel, scale),
        out_shape=(half, half),
        in_specs=[vmem],
        out_specs=(vmem, vmem),
        scratch_shapes=[pltpu.VMEM((order, order), jnp.float32)],
        compiler_params=pltpu.CompilerParams(vmem_limit_bytes=40 * 2**20),
        cost_estimate=pl.CostEstimate(
            flops=400 * order**3 // 10, bytes_accessed=8 * order**2, transcendentals=0
        ),
        name="inverse_cholesky",
    )(product)


def shards(wavefunction, diag_scale, sector_dims, left_ops, right_ops, weight_index, weight_table):
    psi_local = wavefunction[0]
    rows_dev = psi_local.shape[0]
    order_k = psi_local.shape[1]
    pair_count = left_ops.shape[1]
    owners = lax.axis_size("ops")
    first_row = lax.axis_index("ops") * rows_dev
    dim = sector_dims[0]
    live = jnp.arange(order_k) < dim
    both = live[:, None] & live[None, :]
    whole_psi = lax.all_gather(psi_local, "ops", axis=0, tiled=True)
    whole_psi = jnp.where(both, whole_psi, jnp.zeros_like(whole_psi))
    onehot = (weight_index[0][:, None] == jnp.arange(weight_table.shape[0])[None, :]).astype(
        jnp.float32
    )
    coef = jnp.sum(onehot * weight_table[None, :], axis=1)

    total = jnp.zeros((order_k, order_k), jnp.float32)
    operator = jnp.zeros((order_k, order_k), jnp.float32)
    for pair in range(pair_count):
        applied = jnp.dot(
            left_ops[0, pair], whole_psi, preferred_element_type=jnp.float32
        ).astype(jnp.bfloat16)
        term = lax.dot_general(
            applied,
            right_ops[0, pair],
            (((1,), (1,)), ((), ())),
            preferred_element_type=jnp.float32,
        )
        total = total + coef[pair] * term
        operator = operator + coef[pair] * left_ops[0, pair].astype(jnp.float32)
    total = jnp.where(both, total, jnp.float32(0.0))
    whole_f = whole_psi.astype(jnp.float32)
    partial_numer = jnp.sum(whole_f * total)
    denom = jnp.sum(whole_f * whole_f)
    packed = jnp.concatenate(
        [
            total.reshape(owners, rows_dev, order_k),
            jnp.full((owners, SUB, order_k), partial_numer),
        ],
        axis=1,
    ).reshape(owners * (rows_dev + SUB), order_k)
    summed = lax.psum_scatter(packed, "ops", scatter_dimension=0, tiled=True)
    sigma = summed[:rows_dev]
    energy = summed[rows_dev, 0] / denom

    row_live = first_row + jnp.arange(rows_dev) < dim
    psi_f = jnp.where(row_live[:, None] & live[None, :], psi_local, 0).astype(jnp.float32)
    update = psi_f + (sigma - energy * psi_f) / diag_scale[0]
    columns = lax.all_gather(update.astype(jnp.bfloat16), "ops", axis=0, tiled=True)

    operator, columns = lax.optimization_barrier((operator.astype(jnp.bfloat16), columns))
    operator = lax.psum(operator, "ops")

    product = lax.dot_general(
        columns, columns, (((0,), (0,)), ((), ())), preferred_element_type=jnp.float32
    )
    high, low = inverse_cholesky(product, 1.0 / order_k)
    across = (((1,), (1,)), ((), ()))
    basis = (
        lax.dot_general(columns, high, across, preferred_element_type=jnp.float32)
        + lax.dot_general(columns, low, across, preferred_element_type=jnp.float32)
    ).astype(jnp.bfloat16)
    basis_local = lax.dynamic_slice_in_dim(basis, first_row, rows_dev, axis=0)

    own = lax.dynamic_slice_in_dim(basis, first_row, rows_dev, axis=1)
    half = lax.dot_general(
        own, operator, (((0,), (0,)), ((), ())), preferred_element_type=jnp.float32
    ).astype(jnp.bfloat16)
    rotated = jnp.dot(half, basis, preferred_element_type=jnp.float32) / order_k
    next_rows = lax.psum(rotated.astype(jnp.bfloat16), "sector").astype(jnp.float32)
    return (basis_local[None], jnp.reshape(energy, (1,)), next_rows)


def solution(mesh):
    in_specs = (
        P("sector", "ops", None),
        P("sector", "ops", None),
        P("sector"),
        P("sector", "ops", None, None),
        P("sector", "ops", None, None),
        P("sector", "ops"),
        P(),
    )
    out_specs = (P("sector", "ops", None), P("sector"), P("ops", None))
    return jax.shard_map(shards, mesh=mesh, in_specs=in_specs, out_specs=out_specs, check_vma=False)
```

profile of v0, /device:TPU:0, one launch (start us, length us, event | category | flops | bytes accessed | tf_op | source)
XLA Modules:
  0.0 384.1 jit_solution(1623291549600917774)
XLA Ops:
  7.2 0.0 all-gather.6.cloned.1.call-start
  7.2 0.7 all-gather.6.cloned.1.call-update
  7.9 0.0 reduce-scatter.2.cloned.1.call-start
  8.6 0.9 fusion.29
  9.5 0.7 fusion.32
  10.1 51.8 %all-gather.6.cloned.1.call-done = bf16[1,1024,1024]{2,1,0:T(8,128)(2,1)} async-done(((bf16[1,128,1024]{2,1,0:T(8,128)(2,1)}), bf16[1,1024,1024]{2,1,0:T(8,128)(2,1)}) %all-gather.6.cloned.1.call-update) | async-done | bytes 2097168 | tf_op jit(solution)/shard_map/all_gather | solution.py:151
  61.9 0.0 copy-start.4
  61.9 9.8 %fusion.3 = f32[1024,1024]{1,0:T(8,128)} fusion(bf16[1,2,1024,1024]{3,2,1,0:T(8,128)(2,1)} %param.11, bf16[1,2,1024,1024]{3,2,1,0:T(8,128)(2,1)} %param.10, bf16[1,1024,1024]{2,1,0:T(8,128)(2,1)} %all-gather.6.cloned.1.call-done, pred[1024]{0:T(1024)(128)(4,1)S(1)} %iota_compare_fusion), kind=kOutput, calls=%fused_computation.9 | convolution fusion | flops 4298113024 | bytes 10487808 | tf_op jit(solution)/shard_map/dot_general | solution.py:164
  71.7 0.0 copy-done.4
  71.7 13.5 %fusion.1 = (f32[]{:T(128)}, f32[]{:T(128)}, f32[1024,1024]{1,0:T(8,128)}) fusion(bf16[1,1024,1024]{2,1,0:T(8,128)(2,1)S(1)} %copy-done.4, pred[1024]{0:T(1024)(128)(4,1)S(1)} %iota_compare_fusion, bf16[1,2,1024,1024]{3,2,1,0:T(8,128)(2,1)} %param.11, bf16[1,2,1024,1024]{3,2,1,0:T(8,128)(2,1)} %param.10, f32[]{:T(128)} %bitcast.3, f32[1024,1024]{1,0:T(8,128)} %fusion.3, ...), kind=kOutput, calls=%fused_computation.5 | convolution fusion | flops 4309647360 | bytes 16782344 | tf_op jit(solution)/shard_map/dot_general | solution.py:164
  85.3 5.4 %concatenate.3 = f32[8,136,1024]{2,1,0:T(8,128)} pad(f32[8,128,1024]{2,1,0:T(8,128)} %bitcast.65, f32[]{:T(128)} %get-tuple-element.12), padding=0_0x0_8x0_0 | pad | bytes 8650756 | tf_op jit(solution)/shard_map/concatenate | solution.py:176
  90.6 0.0 copy-start
  90.6 0.0 copy-start.1
  90.6 0.0 reduce-scatter.2.cloned.1.call-update
  90.7 0.0 all-gather.4.cloned.1.call-start
  90.7 90.6 %reduce-scatter.2.cloned.1.call-done = f32[136,1024]{1,0:T(8,128)} async-done(((f32[1088,1024]{1,0:T(8,128)}), f32[136,1024]{1,0:T(8,128)}) %reduce-scatter.2.cloned.1.call-update) | async-done | bytes 557072 | tf_op jit(solution)/shard_map/reduce_scatter | solution.py:183
  181.4 1.2 slice.37
  183.9 0.0 copy-done
  183.9 0.0 copy-done.1
  183.9 2.0 fusion.26
  185.9 0.0 all-gather.4.cloned.1.call-update
  185.9 0.2 all-reduce.4.cloned.1.call-start
  186.1 5.9 %add_convert_fusion.1 = bf16[1024,1024]{1,0:T(8,128)(2,1)} fusion(f32[]{:T(128)} %bitcast.3, f32[]{:T(128)} %bitcast.1, bf16[1,2,1024,1024]{3,2,1,0:T(8,128)(2,1)} %param.10), kind=kLoop, calls=%fused_computation.7 | loop fusion | flops 6291456 | bytes 6291464 | tf_op jit(solution)/shard_map/convert_element_type | solution.py:192
  192.0 42.8 %all-gather.4.cloned.1.call-done = bf16[1024,1024]{1,0:T(8,128)(2,1)} async-done(((bf16[128,1024]{1,0:T(8,128)(2,1)}), bf16[1024,1024]{1,0:T(8,128)(2,1)}) %all-gather.4.cloned.1.call-update) | async-done | bytes 2097168 | tf_op jit(solution)/shard_map/all_gather | solution.py:190
  234.8 0.0 copy-start.2
  234.8 0.0 all-reduce.4.cloned.1.call-update
  234.8 0.0 all-reduce.6.cloned.1.call-start
  234.9 1.5 copy-done.2
  236.4 2.4 fusion.35.gram_ref
  238.8 71.6 %inverse_cholesky.1 = (bf16[1024,1024]{1,0:T(8,128)(2,1)S(1)}, bf16[1024,1024]{1,0:T(8,128)(2,1)S(1)}) custom-call(f32[1024,1024]{1,0:T(8,128)S(1)} %fusion.35.gram_ref), custom_call_target="tpu_custom_call" | custom-call | flops 42949672960 | bytes 8388608 | tf_op jit(solution)/shard_map/inverse_cholesky/pallas_call | solution.py:127
  310.3 0.0 copy-start.3
  310.3 2.4 fusion.36
  312.7 0.0 copy-done.3
  312.7 2.4 add_convert_fusion
  315.1 24.7 %all-reduce.4.cloned.1.call-done = bf16[1024,1024]{1,0:T(8,128)(2,1)} async-done(((bf16[1024,1024]{1,0:T(8,128)(2,1)}), bf16[1024,1024]{1,0:T(8,128)(2,1)}) %all-reduce.4.cloned.1.call-update) | async-done | bytes 2097168 | tf_op jit(solution)/shard_map/psum | solution.py:193
  339.8 3.1 fusion.15
  342.9 0.0 all-reduce.6.cloned.1.call-update
  342.9 0.7 dynamic-slice_bitcast_fusion
  343.7 31.0 %all-reduce.6.cloned.1.call-done = bf16[128,1024]{1,0:T(8,128)(2,1)} async-done(((bf16[128,1024]{1,0:T(8,128)(2,1)}), bf16[128,1024]{1,0:T(8,128)(2,1)}) %all-reduce.6.cloned.1.call-update) | async-done | bytes 262160 | tf_op jit(solution)/shard_map/psum | solution.py:211
  374.7 1.8 convert_element_type.52
  (2 shorter events, 0.0 us)
Async XLA Ops:
  7.2 54.8 %all-gather.6.cloned.1.call-start = ((), (), s32[]{:S(2)}) async-start(), calls=%async_computation.5 | async-start | bytes 2359296 | tf_op jit(solution)/shard_map/all_gather | solution.py:151
  7.9 173.5 %reduce-scatter.2.cloned.1.call-start = ((), (), s32[]{:S(2)}) async-start(), calls=%async_computation.1 | async-start | bytes 5013504 | tf_op jit(solution)/shard_map/reduce_scatter | solution.py:183
  61.9 9.8 %copy-start.4 = (bf16[1,1024,1024]{2,1,0:T(8,128)(2,1)S(1)}, bf16[1,1024,1024]{2,1,0:T(8,128)(2,1)}, u32[]{:S(2)}) copy-start(bf16[1,1024,1024]{2,1,0:T(8,128)(2,1)} %all-gather.6.cloned.1.call-done) | copy-start | bytes 6291460
  90.6 93.2 %copy-start = (bf16[1,128,1024]{2,1,0:T(8,128)(2,1)S(1)}, bf16[1,128,1024]{2,1,0:T(8,128)(2,1)}, u32[]{:S(2)}) copy-start(bf16[1,128,1024]{2,1,0:T(8,128)(2,1)} %param.7) | copy-start | bytes 786436
  90.6 93.2 %copy-start.1 = (f32[1,128,1024]{2,1,0:T(8,128)S(1)}, f32[1,128,1024]{2,1,0:T(8,128)}, u32[]{:S(2)}) copy-start(f32[1,128,1024]{2,1,0:T(8,128)} %param.8) | copy-start | bytes 1572868
  90.7 144.1 %all-gather.4.cloned.1.call-start = ((), (), s32[]{:S(2)}) async-start(), calls=%async_computation.2 | async-start | bytes 2359296 | tf_op jit(solution)/shard_map/all_gather | solution.py:190
  185.9 153.9 %all-reduce.4.cloned.1.call-start = ((), (), s32[]{:S(2)}) async-start(), calls=%async_computation.3 | async-start | bytes 4194304 | tf_op jit(solution)/shard_map/psum | solution.py:193
  234.8 1.6 copy-start.2
  234.8 139.8 %all-reduce.6.cloned.1.call-start = ((), (), s32[]{:S(2)}) async-start(), calls=%async_computation.4 | async-start | bytes 524288 | tf_op jit(solution)/shard_map/psum | solution.py:211
  310.3 2.4 copy-start.3
Sparse Core Ops, SparseCore 0:
  10.1 51.7 all-gather.5
  90.8 90.5 reduce-scatter.1
  186.0 48.7 all-gather.3
  238.3 101.4 all-reduce.3
  343.1 31.5 all-reduce.5
where the time goes:
time: 385 us; the launch traced here: 384 us
  waiting for transfers between devices  242 us (63%)
  Pallas kernels  71.6 us (19%)
  matrix products  33.6 us (9%)
  between operations  17 us (4%)
  other arithmetic  10.5 us (3%)
  local copies, waits for them, and re-layouts  9.46 us (2%)
    reduce_scatter x1, waiting for transfers between devices, shards(): summed = lax.psum_scatter(packed, 'ops', scatter_dimension=0, tiled=True)  90.6 us
    pallas_call x1, Pallas kernels, inverse_cholesky(): pl.pallas_call(functools.partial(inverse_kernel, scale), out_shape=(half,...  71.6 us
    all_gather x1, waiting for transfers between devices, shards(): whole_psi = lax.all_gather(psi_local, 'ops', axis=0, tiled=True)  51.8 us
    all_gather x1, waiting for transfers between devices, shards(): lax.all_gather(update.astype(jnp.bfloat16), 'ops', axis=0, tiled=True)  42.8 us
    psum x1, waiting for transfers between devices, shards(): lax.psum(rotated.astype(jnp.bfloat16), 'sector').astype(jnp.float32)  31 us
    psum x1, waiting for transfers between devices, shards(): operator = lax.psum(operator, 'ops')  24.7 us
    dot_general x2, matrix products, shards(): lax.dot_general(applied, right_ops[0, pair], (((1,), (1,)), ((), ())), pr...  23.3 us
  transfers between devices with their start and end apart: 5, of which 5 were waited for; matrix products, arithmetic and copies ran while one was open for 4% of the time, Pallas kernels for 19%

commit v1 on v0

v1 whole, which is shorter than its diff:
```python
import functools

import jax
import jax.numpy as jnp
from jax import lax
from jax.experimental import pallas as pl
from jax.experimental.pallas import tpu as pltpu
from jax.sharding import PartitionSpec as P

BLOCK = 128
SUB = 8
MESH = pl.DeviceIdType.MESH
VMEM_LIMIT = 60 * 2**20
F32 = jnp.float32
BF16 = jnp.bfloat16


def split3(u):
    high = u.astype(jnp.bfloat16).astype(jnp.float32)
    rest = u - high
    mid = rest.astype(jnp.bfloat16).astype(jnp.float32)
    low = (rest - mid).astype(jnp.bfloat16).astype(jnp.float32)
    return high, mid, low


def inverse_factor(block):
    size = block.shape[0]
    lane = lax.broadcasted_iota(jnp.int32, (SUB, size), 1)
    row = lax.broadcasted_iota(jnp.int32, (SUB, size), 0)
    below = block
    done = []
    for s in range(size // SUB):
        at = s * SUB
        top = below[:SUB]
        columns = [
            jnp.broadcast_to(top[:, at + j : at + j + 1], (SUB, size)) for j in range(SUB)
        ]
        here = (lane >= at) & (lane < at + SUB)
        body = jnp.where(here, (lane - at == row).astype(jnp.float32), top)
        pivots = jnp.ones((SUB, size), jnp.float32)
        for j in range(SUB):
            pivot = jnp.broadcast_to(columns[j][j : j + 1], (SUB, size))
            pivots = jnp.where(row == j, pivot, pivots)
            if j < SUB - 1:
                factor = jnp.where(row > j, columns[j] / pivot, 0.0)
                for c in range(j + 1, SUB):
                    columns[c] = columns[c] - factor * columns[c][j : j + 1]
                body = body - factor * body[j : j + 1]
        scaled = body * lax.rsqrt(pivots)
        done.append(scaled)
        if at + SUB < size:
            high, mid, low = split3(scaled)
            left = jnp.concatenate([high, high, mid, high, mid, low], axis=0)
            right = jnp.concatenate([high, mid, high, low, mid, high], axis=0)
            outer = lax.dot_general(
                left.T.astype(jnp.bfloat16),
                right.astype(jnp.bfloat16),
                (((1,), (0,)), ((), ())),
                preferred_element_type=jnp.float32,
            )
            rows_left = size - at - SUB
            lanes = lax.broadcasted_iota(jnp.int32, (rows_left, size), 1)
            kept = jnp.where((lanes >= at) & (lanes < at + SUB), 0.0, below[SUB:])
            below = kept - outer[at + SUB :]
    whole = jnp.concatenate(done, axis=0)
    r = lax.broadcasted_iota(jnp.int32, (size, size), 0)
    c = lax.broadcasted_iota(jnp.int32, (size, size), 1)
    return jnp.where(c <= r, whole, 0.0)


def place(owners):
    me = lax.axis_index("ops")
    return me, me // 2, lax.rem(me, 2)


def send(src, dst, send_sem, recv_sem, target, axis="ops"):
    return pltpu.make_async_remote_copy(
        src_ref=src,
        dst_ref=dst,
        send_sem=send_sem,
        recv_sem=recv_sem,
        device_id={axis: target},
        device_id_type=MESH,
    )


def greet(owners):
    me, pair, side = place(owners)
    half = owners // 2
    barrier = pltpu.get_barrier_semaphore()
    pl.semaphore_signal(
        barrier, inc=1, device_id={"ops": pair * 2 + 1 - side}, device_id_type=MESH
    )
    for k in range(1, half):
        pl.semaphore_signal(
            barrier,
            inc=1,
            device_id={"ops": lax.rem(pair + k, half) * 2 + side},
            device_id_type=MESH,
        )
    pl.semaphore_wait(barrier, half)


def gather_start(owners, own, blocks, send_sem, recv_sem):
    me, pair, side = place(owners)
    half = owners // 2
    for k in range(1, half):
        target = lax.rem(pair + k, half) * 2 + side
        send(own, blocks.at[me], send_sem.at[k], recv_sem.at[me], target).start()
    send(own, blocks.at[me], send_sem.at[0], recv_sem.at[me], pair * 2 + 1 - side).start()


def gather_receive(owners, own, blocks, send_sem, recv_sem, source):
    me, pair, side = place(owners)
    send(own, blocks.at[source], send_sem.at[0], recv_sem.at[source], me).wait_recv()


def gather_pass_on(owners, k, own, blocks, send_sem, recv_sem):
    me, pair, side = place(owners)
    half = owners // 2
    source = lax.rem(pair - k + half, half) * 2 + side
    gather_receive(owners, own, blocks, send_sem, recv_sem, source)
    send(
        blocks.at[source],
        blocks.at[source],
        send_sem.at[half - 1 + k],
        recv_sem.at[source],
        pair * 2 + 1 - side,
    ).start()
    return source


def gather_partner(owners, k, own, blocks, send_sem, recv_sem):
    me, pair, side = place(owners)
    half = owners // 2
    source = lax.rem(pair - k + half, half) * 2 + 1 - side
    gather_receive(owners, own, blocks, send_sem, recv_sem, source)
    return source


def gather_finish(owners, own, blocks, send_sem, recv_sem):
    me, pair, side = place(owners)
    for k in range(owners - 1):
        send(own, blocks.at[me], send_sem.at[k], recv_sem.at[me], me).wait_send()


def sigma_kernel(
    owners,
    psi_ref,
    diag_ref,
    dim_ref,
    index_ref,
    table_ref,
    left_hbm,
    right_hbm,
    columns_hbm,
    gram_ref,
    energy_ref,
    operator_ref,
    left,
    right,
    psi_all,
    psi_live,
    turned,
    sums,
    pair_out,
    pair_in,
    cross_out,
    cross_in,
    number,
    own,
    columns,
    load_sem,
    a_send,
    a_recv,
    p_send,
    p_recv,
    c_send,
    c_recv,
    n_send,
    n_recv,
    x_send,
    x_recv,
    store_sem,
):
    me, pair, side = place(owners)
    half = owners // 2
    partner = pair * 2 + 1 - side
    rows, order = psi_ref.shape
    pairs = left.shape[0]
    dim = dim_ref[0]
    coef = [table_ref[index_ref[0, p]] for p in range(pairs)]

    loads = [pltpu.make_async_copy(right_hbm.at[0], right, load_sem.at[0])]
    loads.append(pltpu.make_async_copy(left_hbm.at[0], left, load_sem.at[1]))
    for load in loads:
        load.start()
    greet(owners)
    gather = (owners, psi_ref, psi_all, a_send, a_recv)
    gather_start(*gather)

    lane = lax.broadcasted_iota(jnp.int32, (rows, order), 1)
    row = lax.broadcasted_iota(jnp.int32, (rows, order), 0)

    def masked(block, owner):
        return jnp.where((lane < dim) & (row + owner * rows < dim), block, jnp.zeros_like(block))

    def turn(block, owner):
        live = masked(block, owner)
        psi_live[owner] = live
        for p in range(pairs):
            turned[p, pl.ds(pl.multiple_of(owner * rows, rows), rows), :] = (
                coef[p]
                * lax.dot_general(
                    live, right[p], (((1,), (1,)), ((), ())), preferred_element_type=F32
                )
            ).astype(BF16)

    loads[0].wait()
    turn(psi_ref[...], me)

    def arrive(k, carry):
        source = gather_pass_on(owners, k, *gather[1:])
        turn(psi_all[source], source)
        source = gather_partner(owners, k - 1, *gather[1:])
        turn(psi_all[source], source)
        return carry

    lax.fori_loop(1, half, arrive, 0)
    source = gather_partner(owners, half - 1, *gather[1:])
    turn(psi_all[source], source)
    loads[1].wait()

    def partial(k, numer):
        at = lax.rem(pair + k, half)
        here = pl.ds(pl.multiple_of(at * 2 * rows, 2 * rows), 2 * rows)
        total = jnp.dot(left[0, here, :], turned[0], preferred_element_type=F32)
        for p in range(1, pairs):
            total += jnp.dot(left[p, here, :], turned[p], preferred_element_type=F32)
        sums[k - 1] = total.reshape(2, rows, order)
        pair_out[k - 1] = sums[k - 1, 1 - side].astype(BF16)
        send(
            pair_out.at[k - 1],
            pair_in.at[k - 1],
            p_send.at[k - 1],
            p_recv.at[k - 1],
            partner,
        ).start()
        for j in range(2):
            product = psi_live[at * 2 + j].astype(F32) * sums[k - 1, j]
            numer = numer + jnp.sum(product.reshape(rows // 8, 8, order), axis=0)
        return numer

    numer = lax.fori_loop(1, half + 1, partial, jnp.zeros((8, order), F32))
    number[0] = jnp.full((8, 128), jnp.sum(numer), F32)
    send(number.at[0], number.at[1], n_send.at[0], n_recv.at[0], partner).start()

    def operate(i, carry):
        here = pl.ds(pl.multiple_of(i * 128, 128), 128)
        total = coef[0] * left[0, here, :].astype(F32)
        for p in range(1, pairs):
            total += coef[p] * left[p, here, :].astype(F32)
        operator_ref[here, :] = total.astype(BF16)
        return carry

    lax.fori_loop(0, order // 128, operate, 0)

    def square(i, carry):
        live = psi_live[i].astype(F32)
        return carry + jnp.sum((live * live).reshape(rows // 8, 8, order), axis=0)

    denom = jnp.sum(lax.fori_loop(0, owners, square, jnp.zeros((8, order), F32)))

    send(number.at[0], number.at[1], n_send.at[0], n_recv.at[0], partner).wait_recv()
    number[2 + pair] = number[0] + number[1]
    for k in range(1, half):
        send(
            number.at[2 + pair],
            number.at[2 + pair],
            n_send.at[k],
            n_recv.at[1 + pair],
            lax.rem(pair + k, half) * 2 + side,
        ).start()

    def crossing(k):
        return send(
            cross_out.at[k - 1],
            cross_in.at[k - 1],
            c_send.at[k - 1],
            c_recv.at[k - 1],
            lax.rem(pair + k, half) * 2 + side,
        )

    def pairing(k):
        return send(
            pair_out.at[k - 1], pair_in.at[k - 1], p_send.at[k - 1], p_recv.at[k - 1], partner
        )

    def cross(k, carry):
        pairing(k).wait_recv()
        cross_out[k - 1] = (sums[k - 1, side] + pair_in[k - 1].astype(F32)).astype(BF16)
        crossing(k).start()
        return carry

    lax.fori_loop(1, half, cross, 0)
    for k in range(1, half):
        source = lax.rem(pair + k, half)
        send(
            number.at[2 + pair], number.at[2 + source], n_send.at[k], n_recv.at[1 + source], me
        ).wait_recv()
    energy = number[2]
    for i in range(1, half):
        energy = energy + number[2 + i]
    energy = energy / denom
    energy_ref[...] = energy
    energy = jnp.max(energy)

    pairing(half).wait_recv()
    total = sums[half - 1, side] + pair_in[half - 1].astype(F32)
    sums[half - 1, side] = total

    def take(k, carry):
        crossing(k).wait_recv()
        sums[half - 1, side] += cross_in[k - 1].astype(F32)
        return carry

    lax.fori_loop(1, half, take, 0)
    sigma = masked(sums[half - 1, side], me)
    psi = psi_live[me].astype(F32)
    own[...] = (psi + (sigma - energy * psi) / diag_ref[...]).astype(BF16)
    gather = (owners, own, columns, x_send, x_recv)
    gather_start(*gather)

    step = 256

    def square_up(block, first):
        for i in range(0, order, step):
            part = lax.dot_general(
                block[:, i : i + step],
                block[:, i:],
                (((0,), (0,)), ((), ())),
                preferred_element_type=F32,
            )
            if first:
                gram_ref[i : i + step, i:] = part
            else:
                gram_ref[i : i + step, i:] += part

    columns[me] = own[...]
    square_up(own[...], True)

    def meet(k, carry):
        one = gather_pass_on(owners, k, *gather[1:])
        two = gather_partner(owners, k - 1, *gather[1:])
        square_up(jnp.concatenate([columns[one], columns[two]], axis=0), False)
        return carry

    lax.fori_loop(1, half, meet, 0)
    last = gather_partner(owners, half - 1, *gather[1:])
    store = pltpu.make_async_copy(columns, columns_hbm, store_sem.at[0])
    store.start()
    square_up(columns[last], False)

    gather_finish(*gather)
    gather_finish(owners, psi_ref, psi_all, a_send, a_recv)
    for k in range(1, half + 1):
        pairing(k).wait_send()
    for k in range(1, half):
        crossing(k).wait_send()
    for k in range(half):
        send(number.at[0], number.at[1], n_send.at[k], n_recv.at[0], partner).wait_send()
    store.wait()


def sigma_stage(psi, diag, dim, left, right, index, table):
    owners = lax.axis_size("ops")
    half = owners // 2
    rows, order = psi.shape
    pairs = left.shape[1]
    vmem = pl.BlockSpec(memory_space=pltpu.VMEM)
    smem = pl.BlockSpec(memory_space=pltpu.SMEM)
    hbm = pl.BlockSpec(memory_space=pl.ANY)
    dma = pltpu.SemaphoreType.DMA
    return pl.pallas_call(
        functools.partial(sigma_kernel, owners),
        out_shape=(
            jax.ShapeDtypeStruct((owners, rows, order), BF16),
            jax.ShapeDtypeStruct((order, order), F32),
            jax.ShapeDtypeStruct((8, 128), F32),
            jax.ShapeDtypeStruct((order, order), BF16),
        ),
        in_specs=[vmem, vmem, smem, smem, smem, hbm, hbm],
        out_specs=(hbm, vmem, vmem, vmem),
        scratch_shapes=[
            pltpu.VMEM((pairs, order, order), BF16),
            pltpu.VMEM((pairs, order, order), BF16),
            pltpu.VMEM((owners, rows, order), BF16),
            pltpu.VMEM((owners, rows, order), BF16),
            pltpu.VMEM((pairs, order, order), BF16),
            pltpu.VMEM((half, 2, rows, order), F32),
            pltpu.VMEM((half, rows, order), BF16),
            pltpu.VMEM((half, rows, order), BF16),
            pltpu.VMEM((half, rows, order), BF16),
            pltpu.VMEM((half, rows, order), BF16),
            pltpu.VMEM((2 + half, 8, 128), F32),
            pltpu.VMEM((rows, order), BF16),
            pltpu.VMEM((owners, rows, order), BF16),
            dma((2,)),
            dma((owners,)),
            dma((owners,)),
            dma((half,)),
            dma((half,)),
            dma((half,)),
            dma((half,)),
            dma((half,)),
            dma((half + 1,)),
            dma((owners,)),
            dma((owners,)),
            dma((1,)),
        ],
        compiler_params=pltpu.CompilerParams(
            collective_id=0, has_side_effects=True, vmem_limit_bytes=VMEM_LIMIT
        ),
        cost_estimate=pl.CostEstimate(
            flops=10 * order**3, bytes_accessed=20 * order**2, transcendentals=0
        ),
        name="sigma_stage",
    )(psi, diag, dim, index, table, left, right)


def inverse_kernel(
    owners,
    scale,
    gram_ref,
    operator_ref,
    high_ref,
    low_ref,
    whole_hbm,
    work,
    pair_in,
    cross_out,
    cross_in,
    own,
    whole,
    p_send,
    p_recv,
    c_send,
    c_recv,
    g_send,
    g_recv,
    store_sem,
):
    me, pair, side = place(owners)
    half = owners // 2
    partner = pair * 2 + 1 - side
    order = gram_ref.shape[0]
    blocks = order // BLOCK
    column = lax.broadcasted_iota(jnp.int32, (BLOCK, order), 1)
    local = lax.broadcasted_iota(jnp.int32, (BLOCK, order), 0)

    def pairing(k):
        return send(
            operator_ref.at[lax.rem(pair + k, half) * 2 + 1 - side],
            pair_in.at[k - 1],
            p_send.at[k - 1],
            p_recv.at[k - 1],
            partner,
        )

    def crossing(k):
        return send(
            cross_out.at[k - 1],
            cross_in.at[k - 1],
            c_send.at[k - 1],
            c_recv.at[k - 1],
            lax.rem(pair + k, half) * 2 + side,
        )

    gather = (owners, own, whole, g_send, g_recv)

    greet(owners)
    for k in range(1, half + 1):
        pairing(k).start()

    def cross():
        def one(k, carry):
            pairing(k).wait_recv()
            at = lax.rem(pair + k, half) * 2 + side
            cross_out[k - 1] = (
                operator_ref[at].astype(F32) + pair_in[k - 1].astype(F32)
            ).astype(BF16)

            @pl.when(k < half)
            def _():
                crossing(k).start()

            return carry

        lax.fori_loop(1, half + 1, one, 0)

    def settle():
        total = cross_out[half - 1].astype(F32)
        for k in range(1, half):
            crossing(k).wait_recv()
            total = total + cross_in[k - 1].astype(F32)
        own[...] = total.astype(BF16)
        gather_start(*gather)
        whole[me] = own[...]

    def hand_on():
        def one(k, carry):
            gather_pass_on(owners, k, *gather[1:])
            return carry

        lax.fori_loop(1, half, one, 0)

    def rows(i):
        return pl.ds(pl.multiple_of(i * BLOCK, BLOCK), BLOCK)

    def load(i, carry):
        eye = (column == local + i * BLOCK).astype(F32)
        work[rows(i), :] = gram_ref[rows(i), :] * scale + 0.001 * eye
        return carry

    lax.fori_loop(0, blocks, load, 0)

    def step(k, carry):
        first = k * BLOCK
        inverse = inverse_factor(work[rows(k), rows(k)])
        in_k = (column >= first) & (column < first + BLOCK)
        pivot_rows = jnp.where(in_k, (column - first == local).astype(F32), work[rows(k), :])
        work[rows(k), :] = jnp.dot(
            inverse, pivot_rows, precision=lax.Precision.HIGHEST, preferred_element_type=F32
        )

        def update(i, inner):
            panel = work[rows(k), rows(i)].T
            kept = jnp.where(in_k, 0.0, work[rows(i), :])
            work[rows(i), :] = kept - jnp.dot(
                panel,
                work[rows(k), :],
                precision=lax.Precision.HIGHEST,
                preferred_element_type=F32,
            )
            return inner

        lax.fori_loop(k + 1, blocks, update, 0)
        pl.when(k == blocks // 4)(cross)
        pl.when(k == blocks // 2)(settle)
        pl.when(k == blocks - 2)(hand_on)
        return carry

    lax.fori_loop(0, blocks, step, 0)

    def receive(k, carry):
        gather_partner(owners, k, *gather[1:])
        return carry

    lax.fori_loop(0, half, receive, 0)
    store_whole = pltpu.make_async_copy(whole, whole_hbm, store_sem.at[0])
    store_whole.start()

    def store(i, carry):
        kept = jnp.where(column <= local + i * BLOCK, work[rows(i), :], 0.0)
        high = kept.astype(BF16)
        high_ref[rows(i), :] = high
        low_ref[rows(i), :] = (kept - high.astype(F32)).astype(BF16)
        return carry

    lax.fori_loop(0, blocks, store, 0)
    gather_finish(*gather)
    for k in range(1, half + 1):
        pairing(k).wait_send()
    for k in range(1, half):
        crossing(k).wait_send()
    store_whole.wait()


def inverse_stage(gram, operator, scale):
    owners = lax.axis_size("ops")
    half_count = owners // 2
    order = gram.shape[0]
    rows = order // owners
    half = jax.ShapeDtypeStruct((order, order), BF16)
    vmem = pl.BlockSpec(memory_space=pltpu.VMEM)
    dma = pltpu.SemaphoreType.DMA
    operator = operator.reshape(owners, rows, order)
    return pl.pallas_call(
        functools.partial(inverse_kernel, owners, scale),
        out_shape=(half, half, jax.ShapeDtypeStruct((owners, rows, order), BF16)),
        in_specs=[vmem, vmem],
        out_specs=(vmem, vmem, pl.BlockSpec(memory_space=pl.ANY)),
        scratch_shapes=[
            pltpu.VMEM((order, order), F32),
            pltpu.VMEM((half_count, rows, order), BF16),
            pltpu.VMEM((half_count, rows, order), BF16),
            pltpu.VMEM((half_count, rows, order), BF16),
            pltpu.VMEM((rows, order), BF16),
            pltpu.VMEM((owners, rows, order), BF16),
            dma((half_count,)),
            dma((half_count,)),
            dma((half_count,)),
            dma((half_count,)),
            dma((owners,)),
            dma((owners,)),
            dma((1,)),
        ],
        compiler_params=pltpu.CompilerParams(
            collective_id=1, has_side_effects=True, vmem_limit_bytes=40 * 2**20
        ),
        cost_estimate=pl.CostEstimate(
            flops=400 * order**3 // 10, bytes_accessed=8 * order**2, transcendentals=0
        ),
        name="inverse_stage",
    )(gram, operator)


def sum_kernel(
    sectors, mine_ref, out_ref, one_out, one_in, two_out, two_in, three_in, sem_send, sem_recv
):
    me = lax.axis_index("sector")
    core = lax.rem(me, 2)
    chip = me // 2
    chips = sectors // 2
    partner = chip * 2 + 1 - core
    rows, order = mine_ref.shape
    part = rows // 2
    barrier = pltpu.get_barrier_semaphore()
    pl.semaphore_signal(barrier, inc=1, device_id={"sector": partner}, device_id_type=MESH)
    for k in range(1, chips):
        pl.semaphore_signal(
            barrier,
            inc=1,
            device_id={"sector": lax.rem(chip + k, chips) * 2 + core},
            device_id_type=MESH,
        )
    pl.semaphore_wait(barrier, chips)

    kept = pl.ds(pl.multiple_of(core * part, part), part)
    given = pl.ds(pl.multiple_of((1 - core) * part, part), part)
    one_out[...] = mine_ref[given, :].astype(BF16)
    first = send(one_out, one_in, sem_send.at[0], sem_recv.at[0], partner, "sector")
    first.start()
    first.wait_recv()
    two_out[...] = (mine_ref[kept, :] + one_in[...].astype(F32)).astype(BF16)
    for k in range(1, chips):
        send(
            two_out,
            two_in.at[chip],
            sem_send.at[k],
            sem_recv.at[1 + chip],
            lax.rem(chip + k, chips) * 2 + core,
            "sector",
        ).start()
    two_in[chip] = two_out[...]
    for k in range(1, chips):
        source = lax.rem(chip + k, chips)
        send(
            two_out, two_in.at[source], sem_send.at[k], sem_recv.at[1 + source], me, "sector"
        ).wait_recv()
    total = two_in[0].astype(F32)
    for i in range(1, chips):
        total = total + two_in[i].astype(F32)
    two_in[0] = total.astype(BF16)
    last = send(two_in.at[0], three_in, sem_send.at[chips], sem_recv.at[chips + 1], partner, "sector")
    last.start()
    out_ref[kept, :] = two_in[0].astype(F32)
    last.wait_recv()
    out_ref[given, :] = three_in[...].astype(F32)
    first.wait_send()
    for k in range(1, chips):
        send(
            two_out, two_in.at[chip], sem_send.at[k], sem_recv.at[1 + chip], me, "sector"
        ).wait_send()
    last.wait_send()


def sum_stage(mine):
    sectors = lax.axis_size("sector")
    chips = sectors // 2
    rows, order = mine.shape
    part = rows // 2
    vmem = pl.BlockSpec(memory_space=pltpu.VMEM)
    dma = pltpu.SemaphoreType.DMA
    return pl.pallas_call(
        functools.partial(sum_kernel, sectors),
        out_shape=jax.ShapeDtypeStruct((rows, order), F32),
        in_specs=[vmem],
        out_specs=vmem,
        scratch_shapes=[
            pltpu.VMEM((part, order), BF16),
            pltpu.VMEM((part, order), BF16),
            pltpu.VMEM((part, order), BF16),
            pltpu.VMEM((chips, part, order), BF16),
            pltpu.VMEM((part, order), BF16),
            dma((chips + 1,)),
            dma((chips + 2,)),
        ],
        compiler_params=pltpu.CompilerParams(collective_id=2, has_side_effects=True),
        cost_estimate=pl.CostEstimate(
            flops=order**2, bytes_accessed=4 * order**2, transcendentals=0
        ),
        name="sum_stage",
    )(mine)


def shards(wavefunction, diag_scale, sector_dims, left_ops, right_ops, weight_index, weight_table):
    rows_dev, order_k = wavefunction.shape[1:]
    first_row = lax.axis_index("ops") * rows_dev
    columns, product, energy, operator = sigma_stage(
        wavefunction[0],
        diag_scale[0],
        sector_dims,
        left_ops,
        right_ops,
        weight_index,
        weight_table,
    )
    high, low, operator = inverse_stage(product, operator, 1.0 / order_k)
    columns = columns.reshape(order_k, order_k)
    operator = operator.reshape(order_k, order_k)
    across = (((1,), (1,)), ((), ()))
    basis = (
        lax.dot_general(columns, high, across, preferred_element_type=F32)
        + lax.dot_general(columns, low, across, preferred_element_type=F32)
    ).astype(BF16)
    basis_local = lax.dynamic_slice_in_dim(basis, first_row, rows_dev, axis=0)
    own = lax.dynamic_slice_in_dim(basis, first_row, rows_dev, axis=1)
    half = lax.dot_general(
        own, operator, (((0,), (0,)), ((), ())), preferred_element_type=F32
    ).astype(BF16)
    rotated = jnp.dot(half, basis, preferred_element_type=F32) / order_k
    next_rows = sum_stage(rotated)
    return (basis_local[None], energy[0, :1], next_rows)


def solution(mesh):
    in_specs = (
        P("sector", "ops", None),
        P("sector", "ops", None),
        P("sector"),
        P("sector", "ops", None, None),
        P("sector", "ops", None, None),
        P("sector", "ops"),
        P(),
    )
    out_specs = (P("sector", "ops", None), P("sector"), P("ops", None))
    return jax.shard_map(shards, mesh=mesh, in_specs=in_specs, out_specs=out_specs, check_vma=False)
```

time: 385 us -> 248 us (0.64)
  the two profiles are of different devices: /device:TPU:0 before, /device:TPU:9 now
where the time goes in v1:
time: 248 us
  Pallas kernels  229 us (92%)
  matrix products  9.39 us (4%)
  local copies, waits for them, and re-layouts  8.53 us (3%)
    pallas_call x1, Pallas kernels, inverse_stage(): pl.pallas_call(functools.partial(inverse_kernel, owners, scale), out_shap...  106 us
    pallas_call x1, Pallas kernels, sigma_stage(): pl.pallas_call(functools.partial(sigma_kernel, owners), out_shape=(jax.Sh...  105 us
    pallas_call x1, Pallas kernels, sum_stage(): pl.pallas_call(functools.partial(sum_kernel, sectors), out_shape=jax.Shap...  17.9 us
    unnamed x7, local copies, waits for them, and re-layouts  5.67 us

profile of v1, /device:TPU:9, one launch (start us, length us, event | category | flops | bytes accessed | tf_op | source)
XLA Modules:
  0.0 248.0 jit_solution(15434951505819234470)
XLA Ops:
  1.3 104.9 %sigma_stage.1 = (bf16[8,128,1024]{2,1,0:T(8,128)(2,1)}, f32[1024,1024]{1,0:T(8,128)}, f32[8,128]{1,0:T(8,128)}, bf16[1024,1024]{1,0:T(8,128)(2,1)}) custom-call(bf16[128,1024]{1,0:T(8,128)(2,1)} %bitcast.17, f32[128,1024]{1,0:T(8,128)} %bitcast.16, s32[1]{0:T(128)S(6)} %copy.11.dim_ref, s32[1,2]{1,0:T(1,128)} %index_ref.1, f32[16]{0:T(128)} %table_ref.1, ...), custom_call_target="tpu_custom_call" | custom-call | flops 10737418240 | bytes 20971520 | tf_op jit(solution)/shard_map/sigma_stage/pallas_call | solution.py:384
  106.2 1.2 slice.3
  107.4 0.0 copy-start
  107.4 1.6 copy-done
  109.0 0.0 copy-start.1
  109.0 2.2 copy-done.1
  111.2 0.0 copy-start.2
  111.2 106.0 %inverse_stage.1 = (bf16[1024,1024]{1,0:T(8,128)(2,1)S(1)}, bf16[1024,1024]{1,0:T(8,128)(2,1)S(1)}, bf16[8,128,1024]{2,1,0:T(8,128)(2,1)S(1)}) custom-call(f32[1024,1024]{1,0:T(8,128)S(1)} %copy-done.1, bf16[8,128,1024]{2,1,0:T(8,128)(2,1)S(1)} %bitcast.15), custom_call_target="tpu_custom_call" | custom-call | flops 42949672960 | bytes 8388608 | tf_op jit(solution)/shard_map/inverse_stage/pallas_call | solution.py:588
  217.1 0.0 copy-done.2
  217.1 2.4 fusion.4
  219.5 3.7 %add_convert_fusion = bf16[1024,1024]{1,0:T(8,128)(2,1)} fusion(f32[1024,1024]{1,0:T(8,128)S(1)} %fusion.4, bf16[1024,1024]{1,0:T(8,128)(2,1)S(1)} %bitcast.19, bf16[1024,1024]{1,0:T(8,128)(2,1)S(1)} %get-tuple-element.14), kind=kOutput, calls=%fused_computation | convolution fusion | flops 2149580800 | bytes 10485760 | tf_op jit(solution)/shard_map/dot_general | solution.py:725
  223.2 3.3 %convolution_multiply_fusion.mine_ref = f32[128,1024]{1,0:T(8,128)} fusion(bf16[1024,1024]{1,0:T(8,128)(2,1)} %add_convert_fusion, bf16[1024,1024]{1,0:T(8,128)(2,1)S(1)} %bitcast.14, s32[]{:T(128)S(6)} %select_n.4), kind=kOutput, calls=%fused_computation.1 | convolution fusion | flops 537133056 | bytes 4980740 | tf_op jit(solution)/shard_map/dot_general | solution.py:732
  226.5 1.7 dynamic-slice_bitcast_fusion
  228.2 17.9 %sum_stage.1 = f32[128,1024]{1,0:T(8,128)} custom-call(f32[128,1024]{1,0:T(8,128)} %convolution_multiply_fusion.mine_ref), custom_call_target="tpu_custom_call" | custom-call | flops 1048576 | bytes 4194304 | tf_op jit(solution)/shard_map/sum_stage/pallas_call | solution.py:685
  246.2 1.9 copy.12
Async XLA Ops:
  107.4 1.6 copy-start
  109.0 2.2 copy-start.1
  111.2 106.0 %copy-start.2 = (bf16[8,128,1024]{2,1,0:T(8,128)(2,1)S(1)}, bf16[8,128,1024]{2,1,0:T(8,128)(2,1)}, u32[]{:S(2)}) copy-start(bf16[8,128,1024]{2,1,0:T(8,128)(2,1)} %get-tuple-element.10) | copy-start | bytes 6291460

commit v2 on v1

v2 whole, which is shorter than its diff:
```python
import functools

import jax
import jax.numpy as jnp
from jax import lax
from jax.experimental import pallas as pl
from jax.experimental.pallas import tpu as pltpu
from jax.sharding import PartitionSpec as P

BLOCK = 128
PANEL = 32
SLAB = 8
MESH = pl.DeviceIdType.MESH
VMEM_LIMIT = 62 * 2**20
F32 = jnp.float32
BF16 = jnp.bfloat16


def split2(u):
    high = u.astype(BF16)
    return high, (u - high.astype(F32)).astype(BF16)


def split3(u):
    high = u.astype(BF16).astype(F32)
    rest = u - high
    mid = rest.astype(BF16).astype(F32)
    low = (rest - mid).astype(BF16).astype(F32)
    return high, mid, low


def inverse_factor(block):
    size = block.shape[0]
    slabs = PANEL // SLAB
    lane = lax.broadcasted_iota(jnp.int32, (SLAB, size), 1)
    row = lax.broadcasted_iota(jnp.int32, (SLAB, size), 0)
    below = block
    done = []
    for at in range(0, size, PANEL):
        top = [below[SLAB * t : SLAB * (t + 1)] for t in range(slabs)]
        columns = {}
        for c in range(PANEL):
            for t in range(c // SLAB, slabs):
                columns[c, t] = jnp.broadcast_to(top[t][:, at + c : at + c + 1], (SLAB, size))
        here = (lane >= at) & (lane < at + PANEL)
        body = [
            jnp.where(here, (lane - at == row + SLAB * t).astype(F32), top[t])
            for t in range(slabs)
        ]
        for j in range(PANEL):
            own, line = j // SLAB, j % SLAB
            root = lax.rsqrt(
                jnp.broadcast_to(columns[j, own][line : line + 1], (SLAB, size))
            )
            scaled = body[own][line : line + 1] * root
            factor = {t: columns[j, t] * root for t in range(own, slabs)}
            for c in range(j + 1, PANEL):
                there = c // SLAB
                across = jnp.broadcast_to(
                    factor[there][c % SLAB : c % SLAB + 1], (SLAB, size)
                )
                for t in range(there, slabs):
                    columns[c, t] = columns[c, t] - factor[t] * across
            under = jnp.where(row > line, factor[own], 0.0)
            body[own] = jnp.where(row == line, scaled, body[own] - under * scaled)
            for t in range(own + 1, slabs):
                body[t] = body[t] - factor[t] * scaled
        whole = jnp.concatenate(body, axis=0)
        done.append(whole)
        if at + PANEL < size:
            high, mid, low = split3(whole)
            left = jnp.concatenate([high, high, mid, high, mid, low], axis=0)
            right = jnp.concatenate([high, mid, high, low, mid, high], axis=0)
            outer = jnp.dot(
                left.T.astype(BF16)[at + PANEL :],
                right.astype(BF16),
                preferred_element_type=F32,
            )
            lanes = lax.broadcasted_iota(jnp.int32, outer.shape, 1)
            kept = jnp.where((lanes >= at) & (lanes < at + PANEL), 0.0, below[PANEL:])
            below = kept - outer
    whole = jnp.concatenate(done, axis=0)
    r = lax.broadcasted_iota(jnp.int32, (size, size), 0)
    c = lax.broadcasted_iota(jnp.int32, (size, size), 1)
    return jnp.where(c <= r, whole, 0.0)


def band(i):
    return slice(i * BLOCK, (i + 1) * BLOCK)


def eliminate(work, k):
    order = work.shape[0]
    blocks = order // BLOCK
    inverse = inverse_factor(work[band(k), band(k)])
    high, low = split2(inverse)
    parts = []
    if k > 0:
        parts.append(work[band(k), : k * BLOCK])
    if k + 1 < blocks:
        parts.append(work[band(k), (k + 1) * BLOCK :])
    rest_high, rest_low = split2(jnp.concatenate(parts, axis=1))
    product = jnp.dot(
        jnp.concatenate([high, high, low], axis=1),
        jnp.concatenate([rest_high, rest_low, rest_high], axis=0),
        preferred_element_type=F32,
    )
    if k > 0:
        work[band(k), : k * BLOCK] = product[:, : k * BLOCK]
    if k + 1 < blocks:
        work[band(k), (k + 1) * BLOCK :] = product[:, k * BLOCK :]
    work[band(k), band(k)] = inverse
    if k + 1 == blocks:
        return
    high, low = split2(work[band(k), :])
    right = jnp.concatenate([high, low, high], axis=0)
    for i in range(k + 1, blocks):
        high, low = split2(work[band(k), band(i)].T)
        left = jnp.concatenate([high, high, low], axis=1)
        change = jnp.dot(left, right[:, : (k + 1) * BLOCK], preferred_element_type=F32)
        if k > 0:
            work[band(i), : k * BLOCK] -= change[:, : k * BLOCK]
        work[band(i), band(k)] = -change[:, k * BLOCK :]
        work[band(i), i * BLOCK :] -= jnp.dot(
            left, right[:, i * BLOCK :], preferred_element_type=F32
        )


def place(owners):
    me = lax.axis_index("ops")
    return me, me // 2, lax.rem(me, 2)


def send(src, dst, send_sem, recv_sem, target, axis="ops"):
    return pltpu.make_async_remote_copy(
        src_ref=src,
        dst_ref=dst,
        send_sem=send_sem,
        recv_sem=recv_sem,
        device_id={axis: target},
        device_id_type=MESH,
    )


def greet(owners, sectors):
    me, pair, side = place(owners)
    half = owners // 2
    here = lax.axis_index("sector")
    chip, core, chips = here // 2, lax.rem(here, 2), sectors // 2
    barrier = pltpu.get_barrier_semaphore()
    targets = [{"ops": pair * 2 + 1 - side}, {"sector": chip * 2 + 1 - core}]
    targets += [{"ops": lax.rem(pair + k, half) * 2 + side} for k in range(1, half)]
    targets += [{"sector": lax.rem(chip + k, chips) * 2 + core} for k in range(1, chips)]
    for target in targets:
        pl.semaphore_signal(barrier, inc=1, device_id=target, device_id_type=MESH)
    pl.semaphore_wait(barrier, half + chips)


def gather_start(owners, own, blocks, send_sem, recv_sem):
    me, pair, side = place(owners)
    half = owners // 2
    for k in range(1, half):
        target = lax.rem(pair + k, half) * 2 + side
        send(own, blocks.at[me], send_sem.at[k], recv_sem.at[me], target).start()
    send(own, blocks.at[me], send_sem.at[0], recv_sem.at[me], pair * 2 + 1 - side).start()


def gather_receive(owners, own, blocks, send_sem, recv_sem, source):
    me, pair, side = place(owners)
    send(own, blocks.at[source], send_sem.at[0], recv_sem.at[source], me).wait_recv()


def gather_pass_on(owners, k, own, blocks, send_sem, recv_sem):
    me, pair, side = place(owners)
    half = owners // 2
    source = lax.rem(pair - k + half, half) * 2 + side
    gather_receive(owners, own, blocks, send_sem, recv_sem, source)
    send(
        blocks.at[source],
        blocks.at[source],
        send_sem.at[half - 1 + k],
        recv_sem.at[source],
        pair * 2 + 1 - side,
    ).start()
    return source


def gather_partner(owners, k, own, blocks, send_sem, recv_sem):
    me, pair, side = place(owners)
    half = owners // 2
    source = lax.rem(pair - k + half, half) * 2 + 1 - side
    gather_receive(owners, own, blocks, send_sem, recv_sem, source)
    return source


def gather_finish(owners, own, blocks, send_sem, recv_sem):
    me, pair, side = place(owners)
    for k in range(owners - 1):
        send(own, blocks.at[me], send_sem.at[k], recv_sem.at[me], me).wait_send()


def step_kernel(
    owners,
    sectors,
    psi_ref,
    diag_ref,
    dim_ref,
    index_ref,
    table_ref,
    left_hbm,
    right_hbm,
    basis_ref,
    energy_ref,
    next_ref,
    left,
    right,
    psi_all,
    psi_live,
    turned,
    sums,
    pair_out,
    pair_in,
    cross_out,
    cross_in,
    number,
    own,
    columns,
    work,
    operator,
    o_pair_in,
    o_cross_out,
    o_cross_in,
    o_own,
    o_whole,
    basis,
    one_out,
    one_in,
    two_out,
    two_in,
    three_in,
    load_sem,
    a_send,
    a_recv,
    p_send,
    p_recv,
    c_send,
    c_recv,
    n_send,
    n_recv,
    x_send,
    x_recv,
    op_send,
    op_recv,
    oc_send,
    oc_recv,
    og_send,
    og_recv,
    s_send,
    s_recv,
):
    me, pair, side = place(owners)
    half = owners // 2
    partner = pair * 2 + 1 - side
    rows, order = psi_ref.shape
    pairs = left.shape[0]
    dim = dim_ref[0]
    coef = [table_ref[index_ref[0, p]] for p in range(pairs)]

    loads = [pltpu.make_async_copy(right_hbm.at[0], right, load_sem.at[0])]
    loads.append(pltpu.make_async_copy(left_hbm.at[0], left, load_sem.at[1]))
    for load in loads:
        load.start()
    greet(owners, sectors)
    gather = (owners, psi_ref, psi_all, a_send, a_recv)
    gather_start(*gather)

    lane = lax.broadcasted_iota(jnp.int32, (rows, order), 1)
    row = lax.broadcasted_iota(jnp.int32, (rows, order), 0)

    def masked(block, owner):
        return jnp.where((lane < dim) & (row + owner * rows < dim), block, jnp.zeros_like(block))

    def turn(block, owner):
        live = masked(block, owner)
        psi_live[owner] = live
        for p in range(pairs):
            turned[p, pl.ds(pl.multiple_of(owner * rows, rows), rows), :] = (
                coef[p]
                * lax.dot_general(
                    live, right[p], (((1,), (1,)), ((), ())), preferred_element_type=F32
                )
            ).astype(BF16)

    loads[0].wait()
    turn(psi_ref[...], me)
    loads[1].wait()

    def operate(i, carry):
        here = pl.ds(pl.multiple_of(i * rows, rows), rows)
        total = coef[0] * left[0, here, :].astype(F32)
        for p in range(1, pairs):
            total += coef[p] * left[p, here, :].astype(F32)
        operator[i] = total.astype(BF16)
        return carry

    lax.fori_loop(0, owners, operate, 0)

    def o_pairing(k):
        return send(
            operator.at[lax.rem(pair + k, half) * 2 + 1 - side],
            o_pair_in.at[k - 1],
            op_send.at[k - 1],
            op_recv.at[k - 1],
            partner,
        )

    def o_crossing(k):
        return send(
            o_cross_out.at[k - 1],
            o_cross_in.at[k - 1],
            oc_send.at[k - 1],
            oc_recv.at[k - 1],
            lax.rem(pair + k, half) * 2 + side,
        )

    def o_pair_sum(k):
        o_pairing(k).wait_recv()
        mine = operator[lax.rem(pair + k, half) * 2 + side]
        return mine.astype(F32) + o_pair_in[k - 1].astype(F32)

    def o_cross(k, carry):
        o_cross_out[k - 1] = o_pair_sum(k).astype(BF16)
        o_crossing(k).start()
        return carry

    def o_start(k, carry):
        o_pairing(k).start()
        return carry

    def arrive(k, carry):
        source = gather_pass_on(owners, k, *gather[1:])
        turn(psi_all[source], source)
        source = gather_partner(owners, k - 1, *gather[1:])
        turn(psi_all[source], source)
        return carry

    lax.fori_loop(1, half, arrive, 0)
    o_pairing(1).start()
    source = gather_partner(owners, half - 1, *gather[1:])
    turn(psi_all[source], source)

    def partial(k, numer):
        at = lax.rem(pair + k, half)
        here = pl.ds(pl.multiple_of(at * 2 * rows, 2 * rows), 2 * rows)
        total = jnp.dot(left[0, here, :], turned[0], preferred_element_type=F32)
        for p in range(1, pairs):
            total += jnp.dot(left[p, here, :], turned[p], preferred_element_type=F32)
        sums[k - 1] = total.reshape(2, rows, order)
        pair_out[k - 1] = sums[k - 1, 1 - side].astype(BF16)
        send(
            pair_out.at[k - 1],
            pair_in.at[k - 1],
            p_send.at[k - 1],
            p_recv.at[k - 1],
            partner,
        ).start()
        for j in range(2):
            product = psi_live[at * 2 + j].astype(F32) * sums[k - 1, j]
            numer = numer + jnp.sum(product.reshape(rows // 8, 8, order), axis=0)
        return numer

    numer = lax.fori_loop(1, half + 1, partial, jnp.zeros((8, order), F32))
    lax.fori_loop(2, half, o_start, 0)
    number[0] = jnp.full((8, 128), jnp.sum(numer), F32)
    send(number.at[0], number.at[1], n_send.at[0], n_recv.at[0], partner).start()

    def square(i, carry):
        live = psi_live[i].astype(F32)
        return carry + jnp.sum((live * live).reshape(rows // 8, 8, order), axis=0)

    denom = jnp.sum(lax.fori_loop(0, owners, square, jnp.zeros((8, order), F32)))

    send(number.at[0], number.at[1], n_send.at[0], n_recv.at[0], partner).wait_recv()
    number[2 + pair] = number[0] + number[1]
    for k in range(1, half):
        send(
            number.at[2 + pair],
            number.at[2 + pair],
            n_send.at[k],
            n_recv.at[1 + pair],
            lax.rem(pair + k, half) * 2 + side,
        ).start()

    def crossing(k):
        return send(
            cross_out.at[k - 1],
            cross_in.at[k - 1],
            c_send.at[k - 1],
            c_recv.at[k - 1],
            lax.rem(pair + k, half) * 2 + side,
        )

    def pairing(k):
        return send(
            pair_out.at[k - 1], pair_in.at[k - 1], p_send.at[k - 1], p_recv.at[k - 1], partner
        )

    def cross(k, carry):
        pairing(k).wait_recv()
        cross_out[k - 1] = (sums[k - 1, side] + pair_in[k - 1].astype(F32)).astype(BF16)
        crossing(k).start()
        return carry

    o_cross(1, 0)
    lax.fori_loop(1, half, cross, 0)
    for k in range(1, half):
        source = lax.rem(pair + k, half)
        send(
            number.at[2 + pair], number.at[2 + source], n_send.at[k], n_recv.at[1 + source], me
        ).wait_recv()
    energy = number[2]
    for i in range(1, half):
        energy = energy + number[2 + i]
    energy = energy / denom
    energy_ref[...] = energy
    energy = jnp.max(energy)

    pairing(half).wait_recv()
    total = sums[half - 1, side] + pair_in[half - 1].astype(F32)
    sums[half - 1, side] = total

    def take(k, carry):
        crossing(k).wait_recv()
        sums[half - 1, side] += cross_in[k - 1].astype(F32)
        return carry

    lax.fori_loop(1, half, take, 0)
    sigma = masked(sums[half - 1, side], me)
    psi = psi_live[me].astype(F32)
    own[...] = (psi + (sigma - energy * psi) / diag_ref[...]).astype(BF16)
    gather = (owners, own, columns, x_send, x_recv)
    gather_start(*gather)

    step = 256

    def square_up(block, first):
        for i in range(0, order, step):
            part = lax.dot_general(
                block[:, i : i + step],
                block[:, i:],
                (((0,), (0,)), ((), ())),
                preferred_element_type=F32,
            )
            if first:
                work[i : i + step, i:] = part
            else:
                work[i : i + step, i:] += part

    columns[me] = own[...]
    square_up(own[...], True)

    def meet(k, carry):
        one = gather_pass_on(owners, k, *gather[1:])
        two = gather_partner(owners, k - 1, *gather[1:])
        square_up(jnp.concatenate([columns[one], columns[two]], axis=0), False)
        return carry

    lax.fori_loop(1, half, meet, 0)
    o_pairing(half).start()
    lax.fori_loop(2, half, o_cross, 0)
    last = gather_partner(owners, half - 1, *gather[1:])
    square_up(columns[last], False)

    o_gather = (owners, o_own, o_whole, og_send, og_recv)

    def o_settle():
        sums[0, 0] = o_pair_sum(half)

        def take(k, carry):
            o_crossing(k).wait_recv()
            sums[0, 0] += o_cross_in[k - 1].astype(F32)
            return carry

        lax.fori_loop(1, half, take, 0)
        o_own[...] = sums[0, 0].astype(BF16)
        gather_start(*o_gather)
        o_whole[me] = o_own[...]

    def o_hand_on(k, carry):
        gather_pass_on(owners, k, *o_gather[1:])
        return carry

    blocks = order // BLOCK
    r = lax.broadcasted_iota(jnp.int32, (BLOCK, BLOCK), 0)
    c = lax.broadcasted_iota(jnp.int32, (BLOCK, BLOCK), 1)
    ridge = jnp.where(r == c, 0.001 * order, 0.0).astype(F32)
    for i in range(blocks):
        work[band(i), band(i)] += ridge
    across = (((1,), (1,)), ((), ()))
    root = order**0.5

    def part_of_basis(rows_of, lines, depth):
        inverse = work[lines, :depth]
        if depth > BLOCK:
            col = lax.broadcasted_iota(jnp.int32, inverse.shape, 1)
            row_at = lax.broadcasted_iota(jnp.int32, inverse.shape, 0) + rows_of
            inverse = jnp.where(col <= row_at, inverse, 0.0)
        high, low = split2(inverse)
        return high, low

    ready = {}
    for k in range(1, half):
        ready.setdefault(blocks // 2 + (k - 1) * (blocks // 2) // max(half - 1, 1), []).append(k)
    for k in range(blocks):
        eliminate(work, k)
        if k == blocks // 4:
            o_settle()
        for j in ready.get(k, []):
            o_hand_on(j, 0)
        if k % 2 == 1:
            depth = (k + 1) * BLOCK
            high, low = part_of_basis(depth - 2 * BLOCK, slice(depth - 2 * BLOCK, depth), depth)
            x = columns[...].reshape(order, order)[:, :depth]
            basis[:, depth - 2 * BLOCK : depth] = (
                (
                    lax.dot_general(x, high, across, preferred_element_type=F32)
                    + lax.dot_general(x, low, across, preferred_element_type=F32)
                )
                * root
            ).astype(BF16)

    first = pl.multiple_of(me * rows, rows)
    mine = pl.ds(first, rows)
    high, low = part_of_basis(first, mine, order)
    x = columns[...].reshape(order, order)
    lines = (
        (
            lax.dot_general(high, x, across, preferred_element_type=F32)
            + lax.dot_general(low, x, across, preferred_element_type=F32)
        )
        * root
    ).astype(BF16)

    def o_partner(k, carry):
        gather_partner(owners, k, *o_gather[1:])
        return carry

    lax.fori_loop(0, half, o_partner, 0)
    turned_lines = jnp.dot(
        lines, o_whole[...].reshape(order, order), preferred_element_type=F32
    ).astype(BF16)
    next_ref[...] = jnp.dot(turned_lines, basis[...], preferred_element_type=F32) / order
    basis_ref[...] = basis[mine, :]
    sum_sectors(sectors, next_ref, one_out, one_in, two_out, two_in, three_in, s_send, s_recv)

    gather_finish(*gather)
    gather_finish(owners, psi_ref, psi_all, a_send, a_recv)
    gather_finish(*o_gather)
    for k in range(1, half + 1):
        pairing(k).wait_send()
        o_pairing(k).wait_send()
    for k in range(1, half):
        crossing(k).wait_send()
        o_crossing(k).wait_send()
    for k in range(half):
        send(number.at[0], number.at[1], n_send.at[k], n_recv.at[0], partner).wait_send()


def sum_sectors(sectors, rows_ref, one_out, one_in, two_out, two_in, three_in, sem_send, sem_recv):
    me = lax.axis_index("sector")
    core = lax.rem(me, 2)
    chip = me // 2
    chips = sectors // 2
    partner = chip * 2 + 1 - core
    rows, order = rows_ref.shape
    part = rows // 2
    kept = pl.ds(pl.multiple_of(core * part, part), part)
    given = pl.ds(pl.multiple_of((1 - core) * part, part), part)
    one_out[...] = rows_ref[given, :].astype(BF16)
    first = send(one_out, one_in, sem_send.at[0], sem_recv.at[0], partner, "sector")
    first.start()
    first.wait_recv()
    two_out[...] = (rows_ref[kept, :] + one_in[...].astype(F32)).astype(BF16)
    for k in range(1, chips):
        send(
            two_out,
            two_in.at[chip],
            sem_send.at[k],
            sem_recv.at[1 + chip],
            lax.rem(chip + k, chips) * 2 + core,
            "sector",
        ).start()
    two_in[chip] = two_out[...]
    for k in range(1, chips):
        source = lax.rem(chip + k, chips)
        send(
            two_out, two_in.at[source], sem_send.at[k], sem_recv.at[1 + source], me, "sector"
        ).wait_recv()
    total = two_in[0].astype(F32)
    for i in range(1, chips):
        total = total + two_in[i].astype(F32)
    two_in[0] = total.astype(BF16)
    last = send(two_in.at[0], three_in, sem_send.at[chips], sem_recv.at[chips + 1], partner, "sector")
    last.start()
    rows_ref[kept, :] = two_in[0].astype(F32)
    last.wait_recv()
    rows_ref[given, :] = three_in[...].astype(F32)
    first.wait_send()
    for k in range(1, chips):
        send(
            two_out, two_in.at[chip], sem_send.at[k], sem_recv.at[1 + chip], me, "sector"
        ).wait_send()
    last.wait_send()


def step_stage(psi, diag, dim, left, right, index, table):
    owners = lax.axis_size("ops")
    sectors = lax.axis_size("sector")
    half, chips = owners // 2, sectors // 2
    rows, order = psi.shape
    pairs = left.shape[1]
    vmem = pl.BlockSpec(memory_space=pltpu.VMEM)
    smem = pl.BlockSpec(memory_space=pltpu.SMEM)
    hbm = pl.BlockSpec(memory_space=pl.ANY)

    def held(*shape):
        return pltpu.VMEM(shape, BF16)

    sems = (2, owners, owners, half, half, half, half, half, half + 1, owners, owners)
    sems += (half, half, half, half, owners, owners, chips + 1, chips + 2)
    return pl.pallas_call(
        functools.partial(step_kernel, owners, sectors),
        out_shape=(
            jax.ShapeDtypeStruct((rows, order), BF16),
            jax.ShapeDtypeStruct((8, 128), F32),
            jax.ShapeDtypeStruct((rows, order), F32),
        ),
        in_specs=[vmem, vmem, smem, smem, smem, hbm, hbm],
        out_specs=(vmem, vmem, vmem),
        scratch_shapes=[
            held(pairs, order, order),
            held(pairs, order, order),
            held(owners, rows, order),
            held(owners, rows, order),
            held(pairs, order, order),
            pltpu.VMEM((half, 2, rows, order), F32),
            held(half, rows, order),
            held(half, rows, order),
            held(half, rows, order),
            held(half, rows, order),
            pltpu.VMEM((2 + half, 8, 128), F32),
            held(rows, order),
            held(owners, rows, order),
            pltpu.VMEM((order, order), F32),
            held(owners, rows, order),
            held(half, rows, order),
            held(half, rows, order),
            held(half, rows, order),
            held(rows, order),
            held(owners, rows, order),
            held(order, order),
            held(rows // 2, order),
            held(rows // 2, order),
            held(rows // 2, order),
            held(chips, rows // 2, order),
            held(rows // 2, order),
        ]
        + [pltpu.SemaphoreType.DMA((n,)) for n in sems],
        compiler_params=pltpu.CompilerParams(
            collective_id=0, has_side_effects=True, vmem_limit_bytes=VMEM_LIMIT
        ),
        cost_estimate=pl.CostEstimate(
            flops=20 * order**3, bytes_accessed=20 * order**2, transcendentals=0
        ),
        name="step_stage",
    )(psi, diag, dim, index, table, left, right)


def shards(wavefunction, diag_scale, sector_dims, left_ops, right_ops, weight_index, weight_table):
    basis, energy, next_rows = step_stage(
        wavefunction[0],
        diag_scale[0],
        sector_dims,
        left_ops,
        right_ops,
        weight_index,
        weight_table,
    )
    return (basis[None], energy[0, :1], next_rows)


def solution(mesh):
    in_specs = (
        P("sector", "ops", None),
        P("sector", "ops", None),
        P("sector"),
        P("sector", "ops", None, None),
        P("sector", "ops", None, None),
        P("sector", "ops"),
        P(),
    )
    out_specs = (P("sector", "ops", None), P("sector"), P("ops", None))
    return jax.shard_map(shards, mesh=mesh, in_specs=in_specs, out_specs=out_specs, check_vma=False)
```

time: 248 us -> 198 us (0.80)
  the two profiles are of different devices: /device:TPU:9 before, /device:TPU:0 now
where the time goes in v2:
time: 198 us; the launch traced here: 197 us
  Pallas kernels  191 us (96%)
  local copies, waits for them, and re-layouts  4.74 us (2%)
    pallas_call x1, Pallas kernels, step_stage(): pl.pallas_call(functools.partial(step_kernel, owners, sectors), out_shape...  191 us

profile of v2, /device:TPU:0, one launch (start us, length us, event | category | flops | bytes accessed | tf_op | source)
XLA Modules:
  0.0 197.4 jit_solution(8111258160983291777)
XLA Ops:
  1.3 191.4 %step_stage.1 = (bf16[128,1024]{1,0:T(8,128)(2,1)}, f32[8,128]{1,0:T(8,128)}, f32[128,1024]{1,0:T(8,128)}) custom-call(bf16[128,1024]{1,0:T(8,128)(2,1)} %bitcast.6, f32[128,1024]{1,0:T(8,128)} %bitcast.5, s32[1]{0:T(128)S(6)} %copy.12.dim_ref, s32[1,2]{1,0:T(1,128)} %index_ref.1, f32[16]{0:T(128)} %table_ref.1, bf16[1,2,1024,1024]{3,2,1,0:T(8,128)(2,1)} %left_hbm.1, ...), custom_call_target="tpu_custom_call" | custom-call | flops 21474836480 | bytes 20971520 | tf_op jit(solution)/shard_map/step_stage/pallas_call | solution.py:631
  192.7 1.2 slice.3
  193.9 1.7 copy.13
  195.5 1.9 copy.14

commit v3 on v2

v3 whole, which is shorter than its diff:
```python
import functools

import jax
import jax.numpy as jnp
from jax import lax
from jax.experimental import pallas as pl
from jax.experimental.pallas import tpu as pltpu
from jax.sharding import PartitionSpec as P

BLOCK = 128
PANEL = 32
SLAB = 8
CHUNKS = 2
MESH = pl.DeviceIdType.MESH
VMEM_LIMIT = 62 * 2**20
F32 = jnp.float32
BF16 = jnp.bfloat16


def split2(u):
    high = u.astype(BF16)
    return high, (u - high.astype(F32)).astype(BF16)


def split3(u):
    high = u.astype(BF16).astype(F32)
    rest = u - high
    mid = rest.astype(BF16).astype(F32)
    low = (rest - mid).astype(BF16).astype(F32)
    return high, mid, low


def inverse_factor(block):
    size = block.shape[0]
    slabs = PANEL // SLAB
    lane = lax.broadcasted_iota(jnp.int32, (SLAB, size), 1)
    row = lax.broadcasted_iota(jnp.int32, (SLAB, size), 0)
    below = block
    done = []
    for at in range(0, size, PANEL):
        top = [below[SLAB * t : SLAB * (t + 1)] for t in range(slabs)]
        columns = {}
        for c in range(PANEL):
            for t in range(c // SLAB, slabs):
                columns[c, t] = jnp.broadcast_to(top[t][:, at + c : at + c + 1], (SLAB, size))
        here = (lane >= at) & (lane < at + PANEL)
        body = [
            jnp.where(here, (lane - at == row + SLAB * t).astype(F32), top[t])
            for t in range(slabs)
        ]
        for j in range(PANEL):
            own, line = j // SLAB, j % SLAB
            root = lax.rsqrt(
                jnp.broadcast_to(columns[j, own][line : line + 1], (SLAB, size))
            )
            scaled = body[own][line : line + 1] * root
            factor = {t: columns[j, t] * root for t in range(own, slabs)}
            for c in range(j + 1, PANEL):
                there = c // SLAB
                across = jnp.broadcast_to(
                    factor[there][c % SLAB : c % SLAB + 1], (SLAB, size)
                )
                for t in range(there, slabs):
                    columns[c, t] = columns[c, t] - factor[t] * across
            under = jnp.where(row > line, factor[own], 0.0)
            body[own] = jnp.where(row == line, scaled, body[own] - under * scaled)
            for t in range(own + 1, slabs):
                body[t] = body[t] - factor[t] * scaled
        whole = jnp.concatenate(body, axis=0)
        done.append(whole)
        if at + PANEL < size:
            high, mid, low = split3(whole)
            left = jnp.concatenate([high, high, mid, high, mid, low], axis=0)
            right = jnp.concatenate([high, mid, high, low, mid, high], axis=0)
            outer = jnp.dot(
                left.T.astype(BF16)[at + PANEL :],
                right.astype(BF16),
                preferred_element_type=F32,
            )
            lanes = lax.broadcasted_iota(jnp.int32, outer.shape, 1)
            kept = jnp.where((lanes >= at) & (lanes < at + PANEL), 0.0, below[PANEL:])
            below = kept - outer
    whole = jnp.concatenate(done, axis=0)
    r = lax.broadcasted_iota(jnp.int32, (size, size), 0)
    c = lax.broadcasted_iota(jnp.int32, (size, size), 1)
    return jnp.where(c <= r, whole, 0.0)


def band(i):
    return slice(i * BLOCK, (i + 1) * BLOCK)


def eliminate(work, k):
    order = work.shape[0]
    blocks = order // BLOCK
    inverse = inverse_factor(work[band(k), band(k)])
    high, low = split2(inverse)
    parts = []
    if k > 0:
        parts.append(work[band(k), : k * BLOCK])
    if k + 1 < blocks:
        parts.append(work[band(k), (k + 1) * BLOCK :])
    rest_high, rest_low = split2(jnp.concatenate(parts, axis=1))
    product = jnp.dot(
        jnp.concatenate([high, high, low], axis=1),
        jnp.concatenate([rest_high, rest_low, rest_high], axis=0),
        preferred_element_type=F32,
    )
    if k > 0:
        work[band(k), : k * BLOCK] = product[:, : k * BLOCK]
    if k + 1 < blocks:
        work[band(k), (k + 1) * BLOCK :] = product[:, k * BLOCK :]
    work[band(k), band(k)] = inverse
    if k + 1 == blocks:
        return
    high, low = split2(work[band(k), :])
    right = jnp.concatenate([high, low, high], axis=0)
    for i in range(k + 1, blocks):
        high, low = split2(work[band(k), band(i)].T)
        left = jnp.concatenate([high, high, low], axis=1)
        change = jnp.dot(left, right[:, : (k + 1) * BLOCK], preferred_element_type=F32)
        if k > 0:
            work[band(i), : k * BLOCK] -= change[:, : k * BLOCK]
        work[band(i), band(k)] = -change[:, k * BLOCK :]
        work[band(i), i * BLOCK :] -= jnp.dot(
            left, right[:, i * BLOCK :], preferred_element_type=F32
        )


def place(owners):
    me = lax.axis_index("ops")
    return me, me // 2, lax.rem(me, 2)


def send(src, dst, send_sem, recv_sem, target, axis="ops"):
    return pltpu.make_async_remote_copy(
        src_ref=src,
        dst_ref=dst,
        send_sem=send_sem,
        recv_sem=recv_sem,
        device_id={axis: target},
        device_id_type=MESH,
    )


def greet(owners, sectors):
    me, pair, side = place(owners)
    half = owners // 2
    here = lax.axis_index("sector")
    chip, core, chips = here // 2, lax.rem(here, 2), sectors // 2
    barrier = pltpu.get_barrier_semaphore()
    targets = [{"ops": pair * 2 + 1 - side}, {"sector": chip * 2 + 1 - core}]
    targets += [{"ops": lax.rem(pair + k, half) * 2 + side} for k in range(1, half)]
    targets += [{"sector": lax.rem(chip + k, chips) * 2 + core} for k in range(1, chips)]
    for target in targets:
        pl.semaphore_signal(barrier, inc=1, device_id=target, device_id_type=MESH)
    pl.semaphore_wait(barrier, half + chips)


def piece(c, order):
    return pl.ds(c * (order // CHUNKS), order // CHUNKS)


def within(value, count):
    return (value >= 0) & (value < count)


def gather_line(owners, own, blocks, send_sem, recv_sem, visit, finish=False):
    me, pair, side = place(owners)
    half = owners // 2
    order = own.shape[1]

    def copy(source_pair, c, way, source=None):
        at = source_pair * 2 + side
        here = blocks.at[at, :, piece(c, order)] if source is None else source
        target = pair * 2 + 1 - side
        if way:
            target = (pair + (1 if way == 1 else -1)) * 2 + side
        return send(
            here,
            blocks.at[at, :, piece(c, order)],
            send_sem.at[(way * half + source_pair) * CHUNKS + c],
            recv_sem.at[at * CHUNKS + c],
            target,
        )

    def arrived(at, c):
        there = blocks.at[at, :, piece(c, order)]
        send(there, there, send_sem.at[0], recv_sem.at[at * CHUNKS + c], me).wait_recv()

    if finish:
        def left_over(p, carry):
            for c in range(CHUNKS):
                copy(p, c, 0).wait_send()

                @pl.when((p <= pair) & (pair < half - 1))
                def _():
                    copy(p, c, 1).wait_send()

                @pl.when((p >= pair) & (pair > 0))
                def _():
                    copy(p, c, 2).wait_send()

            return carry

        lax.fori_loop(0, half, left_over, 0)
        return

    for c in range(CHUNKS):
        mine = own.at[:, piece(c, order)]

        @pl.when(pair < half - 1)
        def _():
            copy(pair, c, 1, mine).start()

        @pl.when(pair > 0)
        def _():
            copy(pair, c, 2, mine).start()

        copy(pair, c, 0, mine).start()

    def hop(d):
        for c in range(CHUNKS):
            for way, source in ((1, pair - d), (2, pair + d)):

                @pl.when(within(source, half))
                def _():
                    arrived(source * 2 + side, c)

                    @pl.when(pair < half - 1 if way == 1 else pair > 0)
                    def _():
                        copy(source, c, way).start()

                    copy(source, c, 0).start()

    def take(d):
        def one(g, carry):
            source = pair + (2 * g - 1) * d

            @pl.when(within(source, half) & (d + g > 0))
            def _():
                for c in range(CHUNKS):
                    arrived(source * 2 + 1 - side, c)
                visit(source)

            return carry

        lax.fori_loop(0, 2, one, 0)

    def step(d, carry):
        hop(d)
        take(d - 1)
        return carry

    lax.fori_loop(1, half + 1, step, 0)


def turn_of(owners, j):
    me, pair, side = place(owners)
    half = owners // 2
    last = j // (half - 1)
    upper = (2 * pair) // half
    down = half - 2 - j + (2 * half - 2 - j - pair) // half
    up = j + (j - pair + half) // half
    return (down * (1 - upper) + up * upper) * (1 - last) + pair * last


def reduce_line(owners, produce, between, sums, pair_out, pair_in, line_out, line_in, sems, finish=False):
    me, pair, side = place(owners)
    half = owners // 2
    order = pair_out.shape[2]
    p_send, p_recv, l_send, l_recv = sems

    def pairing(p, c):
        return send(
            pair_out.at[p, :, piece(c, order)],
            pair_in.at[p, :, piece(c, order)],
            p_send.at[p * CHUNKS + c],
            p_recv.at[p * CHUNKS + c],
            pair * 2 + 1 - side,
        )

    def moving(p, c, way, target):
        return send(
            line_out.at[p, :, piece(c, order)],
            line_in.at[way, p, :, piece(c, order)],
            l_send.at[p * CHUNKS + c],
            l_recv.at[(way * half + p) * CHUNKS + c],
            target,
        )

    if finish:
        def left_over(p, carry):
            for c in range(CHUNKS):
                pairing(p, c).wait_send()

                @pl.when(p != pair)
                def _():
                    moving(p, c, 0, me).wait_send()

            return carry

        lax.fori_loop(0, half, left_over, 0)
        return

    def serve(p):
        produce(p)
        pair_out[p] = sums[p, 1 - side].astype(BF16)
        for c in range(CHUNKS):
            pairing(p, c).start()

    def first(j, carry):
        serve(turn_of(owners, j))
        return carry

    lax.fori_loop(0, half, first, 0)
    between()

    def add(p, c, value):
        sums[p, side, :, piece(c, order)] += value.astype(F32)

    def pass_on(j, carry):
        p = turn_of(owners, j)
        for c in range(CHUNKS):
            pairing(p, c).wait_recv()
            add(p, c, pair_in[p, :, piece(c, order)])
            for way in range(2):
                ahead = p > pair if way == 0 else p < pair
                behind = pair > 0 if way == 0 else pair < half - 1

                @pl.when(ahead & behind)
                def _():
                    moving(p, c, way, me).wait_recv()
                    add(p, c, line_in[way, p, :, piece(c, order)])

            line_out[p, :, piece(c, order)] = sums[p, side, :, piece(c, order)].astype(BF16)
            for way in range(2):

                @pl.when(p > pair if way == 0 else p < pair)
                def _():
                    target = (pair + 1 - 2 * way) * 2 + side
                    moving(p, c, way, target).start()

        return carry

    lax.fori_loop(0, half - 1, pass_on, 0)
    for c in range(CHUNKS):
        pairing(pair, c).wait_recv()
        add(pair, c, pair_in[pair, :, piece(c, order)])
        for way in range(2):

            @pl.when(pair > 0 if way == 0 else pair < half - 1)
            def _():
                moving(pair, c, way, me).wait_recv()
                add(pair, c, line_in[way, pair, :, piece(c, order)])


def step_kernel(
    owners,
    sectors,
    psi_ref,
    diag_ref,
    dim_ref,
    index_ref,
    table_ref,
    left_hbm,
    right_hbm,
    basis_ref,
    energy_ref,
    next_ref,
    left,
    right,
    psi_all,
    psi_live,
    turned,
    sums,
    pair_out,
    pair_in,
    line_out,
    line_in,
    number,
    own,
    columns,
    work,
    operator,
    basis,
    moved,
    core_out,
    core_in,
    core_sums,
    f_pair_out,
    f_pair_in,
    f_line_out,
    f_line_in,
    two_out,
    two_in,
    three_in,
    load_sem,
    a_send,
    a_recv,
    p_send,
    p_recv,
    l_send,
    l_recv,
    n_send,
    n_recv,
    x_send,
    x_recv,
    d_send,
    d_recv,
    fp_send,
    fp_recv,
    fl_send,
    fl_recv,
    s_send,
    s_recv,
):
    me, pair, side = place(owners)
    half = owners // 2
    partner = pair * 2 + 1 - side
    rows, order = psi_ref.shape
    part = rows // 2
    pairs = left.shape[0]
    dim = dim_ref[0]
    coef = [table_ref[index_ref[0, p]] for p in range(pairs)]
    here = lax.axis_index("sector")
    chip, core, chips = here // 2, lax.rem(here, 2), sectors // 2
    core_partner = chip * 2 + 1 - core

    loads = [pltpu.make_async_copy(right_hbm.at[0], right, load_sem.at[0])]
    loads.append(pltpu.make_async_copy(left_hbm.at[0], left, load_sem.at[1]))
    for load in loads:
        load.start()
    greet(owners, sectors)

    def masked(block, first):
        lane = lax.broadcasted_iota(jnp.int32, block.shape, 1)
        row = lax.broadcasted_iota(jnp.int32, block.shape, 0)
        return jnp.where((lane < dim) & (row + first < dim), block, jnp.zeros_like(block))

    def pair_rows(p):
        return pl.ds(pl.multiple_of(p * 2 * rows, 2 * rows), 2 * rows)

    def both(blocks, p):
        return blocks[pl.ds(p * 2, 2)].reshape(2 * rows, order)

    def turn(p):
        live = masked(both(psi_all, p), p * 2 * rows)
        psi_live[pair_rows(p), :] = live
        for i in range(pairs):
            turned[i, pair_rows(p), :] = (
                coef[i]
                * lax.dot_general(
                    live, right[i], (((1,), (1,)), ((), ())), preferred_element_type=F32
                )
            ).astype(BF16)

    psi_all[me] = psi_ref[...]
    loads[0].wait()
    gather_line(owners, psi_ref, psi_all, a_send, a_recv, turn)
    loads[1].wait()

    def partial(p):
        total = jnp.dot(left[0, pair_rows(p), :], turned[0], preferred_element_type=F32)
        for i in range(1, pairs):
            total += jnp.dot(left[i, pair_rows(p), :], turned[i], preferred_element_type=F32)
        sums[p] = total.reshape(2, rows, order)
        product = psi_live[pair_rows(p), :].astype(F32) * sums[p].reshape(2 * rows, order)
        number[0] += fold(product)

    def fold(values):
        tall = jnp.sum(values.reshape(values.shape[0] // 8, 8, order), axis=0)
        total = tall[:, :128]
        for i in range(128, order, 128):
            total = total + tall[:, i : i + 128]
        return total

    number[0] = jnp.zeros((8, 128), F32)
    denoms = []

    def numbers(k, slot, target):
        return send(
            number.at[slot], number.at[slot], n_send.at[k], n_recv.at[slot], target
        )

    def exchange():
        number[2 + me] = number[0]
        for k in range(1, half):
            numbers(k, 2 + me, lax.rem(pair + k, half) * 2 + side).start()
        numbers(0, 2 + me, partner).start()

        def square(i, carry):
            live = psi_live[pl.ds(pl.multiple_of(i * BLOCK, BLOCK), BLOCK), :].astype(F32)
            return carry + fold(live * live)

        denoms.append(
            jnp.sum(lax.fori_loop(0, order // BLOCK, square, jnp.zeros((8, 128), F32)))
        )

        def operate(i, carry):
            at = pl.ds(pl.multiple_of(i * BLOCK, BLOCK), BLOCK)
            total = coef[0] * left[0, at, :].astype(F32)
            for p in range(1, pairs):
                total += coef[p] * left[p, at, :].astype(F32)
            operator[at, :] = total.astype(BF16)
            work[at, :] = jnp.zeros((BLOCK, order), F32)
            return carry

        lax.fori_loop(0, order // BLOCK, operate, 0)
        for k in range(1, half):
            source = lax.rem(pair + k, half) * 2 + side
            numbers(0, 2 + source, me).wait_recv()
            numbers(half - 1 + k, 2 + source, partner).start()

    reduction = (sums, pair_out, pair_in, line_out, line_in, (p_send, p_recv, l_send, l_recv))
    reduce_line(owners, partial, exchange, *reduction)
    for k in range(half):
        numbers(0, 2 + lax.rem(pair + k, half) * 2 + 1 - side, me).wait_recv()
    energy = number[2]
    for i in range(1, owners):
        energy = energy + number[2 + i]
    energy = jnp.full((8, 128), jnp.sum(energy), F32) / denoms[0]
    energy_ref[...] = energy
    energy = jnp.max(energy)

    sigma = masked(sums[pair, side], me * rows)
    psi = psi_live[pl.ds(pl.multiple_of(me * rows, rows), rows), :].astype(F32)
    own[...] = (psi + (sigma - energy * psi) / diag_ref[...]).astype(BF16)
    columns[me] = own[...]

    step = 256

    def square_up(p):
        block = both(columns, p)
        for i in range(0, order, step):
            work[i : i + step, i:] += lax.dot_general(
                block[:, i : i + step],
                block[:, i:],
                (((0,), (0,)), ((), ())),
                preferred_element_type=F32,
            )

    gather_line(owners, own, columns, x_send, x_recv, square_up)

    blocks = order // BLOCK
    r = lax.broadcasted_iota(jnp.int32, (BLOCK, BLOCK), 0)
    c = lax.broadcasted_iota(jnp.int32, (BLOCK, BLOCK), 1)
    ridge = jnp.where(r == c, 0.001 * order, 0.0).astype(F32)
    for i in range(blocks):
        work[band(i), band(i)] += ridge
    across = (((1,), (1,)), ((), ()))
    root = order**0.5
    for k in range(blocks):
        eliminate(work, k)
        if k % 2 == 1:
            depth = (k + 1) * BLOCK
            lines = slice(depth - 2 * BLOCK, depth)
            inverse = work[lines, :depth]
            col = lax.broadcasted_iota(jnp.int32, inverse.shape, 1)
            row = lax.broadcasted_iota(jnp.int32, inverse.shape, 0) + depth - 2 * BLOCK
            high, low = split2(jnp.where(col <= row, inverse, 0.0))
            x = columns[...].reshape(order, order)[:, :depth]
            basis[:, lines] = (
                (
                    lax.dot_general(x, high, across, preferred_element_type=F32)
                    + lax.dot_general(x, low, across, preferred_element_type=F32)
                )
                * root
            ).astype(BF16)
            moved[:, lines] = jnp.dot(
                operator[...], basis[:, lines], preferred_element_type=F32
            ).astype(BF16)

    def swapping(p):
        return send(
            core_out.at[p],
            core_in.at[p],
            d_send.at[p],
            d_recv.at[p],
            core_partner,
            "sector",
        )

    for p in range(half):
        sums[p] = lax.dot_general(
            basis[:, p * 2 * rows : (p + 1) * 2 * rows],
            moved[...],
            (((0,), (0,)), ((), ())),
            preferred_element_type=F32,
        ).reshape(2, rows, order) * (1.0 / order)
        given = sums[p, :, pl.ds(pl.multiple_of((1 - core) * part, part), part), :]
        core_out[p] = given.astype(BF16)
        swapping(p).start()

    def halves(p):
        swapping(p).wait_recv()
        kept = sums[p, :, pl.ds(pl.multiple_of(core * part, part), part), :]
        core_sums[p] = kept + core_in[p].astype(F32)

    last = (
        core_sums,
        f_pair_out,
        f_pair_in,
        f_line_out,
        f_line_in,
        (fp_send, fp_recv, fl_send, fl_recv),
    )
    reduce_line(owners, halves, lambda: None, *last)
    basis_ref[...] = basis[pl.ds(pl.multiple_of(me * rows, rows), rows), :]
    sum_chips(
        chips, core_sums[pair, side], next_ref, two_out, two_in, three_in, s_send, s_recv
    )

    gather_line(owners, psi_ref, psi_all, a_send, a_recv, None, finish=True)
    gather_line(owners, own, columns, x_send, x_recv, None, finish=True)
    reduce_line(owners, None, None, *reduction, finish=True)
    reduce_line(owners, None, None, *last, finish=True)

    def swapped(p, carry):
        swapping(p).wait_send()
        return carry

    lax.fori_loop(0, half, swapped, 0)
    for k in range(owners - 1):
        numbers(k, 2 + me, me).wait_send()


def sum_chips(chips, mine, rows_ref, two_out, two_in, three_in, sem_send, sem_recv):
    here = lax.axis_index("sector")
    chip, core = here // 2, lax.rem(here, 2)
    partner = chip * 2 + 1 - core
    part = mine.shape[0]
    two_out[...] = mine.astype(BF16)
    for k in range(1, chips):
        send(
            two_out,
            two_in.at[chip],
            sem_send.at[k],
            sem_recv.at[1 + chip],
            lax.rem(chip + k, chips) * 2 + core,
            "sector",
        ).start()
    two_in[chip] = two_out[...]
    for k in range(1, chips):
        source = lax.rem(chip + k, chips)
        send(
            two_out, two_in.at[source], sem_send.at[k], sem_recv.at[1 + source], here, "sector"
        ).wait_recv()
    total = two_in[0].astype(F32)
    for i in range(1, chips):
        total = total + two_in[i].astype(F32)
    two_out_sum = total.astype(BF16)
    three_in[core] = two_out_sum
    last = send(
        three_in.at[core],
        three_in.at[core],
        sem_send.at[0],
        sem_recv.at[0],
        partner,
        "sector",
    )
    last.start()
    rows_ref[pl.ds(pl.multiple_of(core * part, part), part), :] = two_out_sum.astype(F32)
    other = send(
        three_in.at[1 - core],
        three_in.at[1 - core],
        sem_send.at[0],
        sem_recv.at[0],
        here,
        "sector",
    )
    other.wait_recv()
    rows_ref[pl.ds(pl.multiple_of((1 - core) * part, part), part), :] = three_in[1 - core].astype(
        F32
    )
    last.wait_send()
    for k in range(1, chips):
        send(
            two_out, two_in.at[chip], sem_send.at[k], sem_recv.at[1 + chip], here, "sector"
        ).wait_send()


def step_stage(psi, diag, dim, left, right, index, table):
    owners = lax.axis_size("ops")
    sectors = lax.axis_size("sector")
    half, chips = owners // 2, sectors // 2
    rows, order = psi.shape
    part = rows // 2
    pairs = left.shape[1]
    vmem = pl.BlockSpec(memory_space=pltpu.VMEM)
    smem = pl.BlockSpec(memory_space=pltpu.SMEM)
    hbm = pl.BlockSpec(memory_space=pl.ANY)

    def held(*shape):
        return pltpu.VMEM(shape, BF16)

    gather = (3 * half * CHUNKS, owners * CHUNKS)
    reduce = (half * CHUNKS, half * CHUNKS, half * CHUNKS, 2 * half * CHUNKS)
    sems = (2,) + gather + reduce + (owners, owners + 2) + gather + (half, half) + reduce
    sems += (chips, chips + 1)
    return pl.pallas_call(
        functools.partial(step_kernel, owners, sectors),
        out_shape=(
            jax.ShapeDtypeStruct((rows, order), BF16),
            jax.ShapeDtypeStruct((8, 128), F32),
            jax.ShapeDtypeStruct((rows, order), F32),
        ),
        in_specs=[vmem, vmem, smem, smem, smem, hbm, hbm],
        out_specs=(vmem, vmem, vmem),
        scratch_shapes=[
            held(pairs, order, order),
            held(pairs, order, order),
            held(owners, rows, order),
            held(order, order),
            held(pairs, order, order),
            pltpu.VMEM((half, 2, rows, order), F32),
            held(half, rows, order),
            held(half, rows, order),
            held(half, rows, order),
            held(2, half, rows, order),
            pltpu.VMEM((2 + owners, 8, 128), F32),
            held(rows, order),
            held(owners, rows, order),
            pltpu.VMEM((order, order), F32),
            held(order, order),
            held(order, order),
            held(order, order),
            held(half, 2, part, order),
            held(half, 2, part, order),
            pltpu.VMEM((half, 2, part, order), F32),
            held(half, part, order),
            held(half, part, order),
            held(half, part, order),
            held(2, half, part, order),
            held(part, order),
            held(chips, part, order),
            held(2, part, order),
        ]
        + [pltpu.SemaphoreType.DMA((n,)) for n in sems],
        compiler_params=pltpu.CompilerParams(
            collective_id=0, has_side_effects=True, vmem_limit_bytes=VMEM_LIMIT
        ),
        cost_estimate=pl.CostEstimate(
            flops=20 * order**3, bytes_accessed=20 * order**2, transcendentals=0
        ),
        name="step_stage",
    )(psi, diag, dim, index, table, left, right)


def shards(wavefunction, diag_scale, sector_dims, left_ops, right_ops, weight_index, weight_table):
    basis, energy, next_rows = step_stage(
        wavefunction[0],
        diag_scale[0],
        sector_dims,
        left_ops,
        right_ops,
        weight_index,
        weight_table,
    )
    return (basis[None], energy[0, :1], next_rows)


def solution(mesh):
    in_specs = (
        P("sector", "ops", None),
        P("sector", "ops", None),
        P("sector"),
        P("sector", "ops", None, None),
        P("sector", "ops", None, None),
        P("sector", "ops"),
        P(),
    )
    out_specs = (P("sector", "ops", None), P("sector"), P("ops", None))
    return jax.shard_map(shards, mesh=mesh, in_specs=in_specs, out_specs=out_specs, check_vma=False)
```

time: 198 us -> 157 us (0.79)
  Pallas kernels: 191 us -> 151 us
    pallas_call x1, Pallas kernels: 191 us -> 151 us  [step_stage(): pl.pallas_call(functools.partial(step_kernel, owners, sectors), out_shape...]
where the time goes in v3:
time: 157 us
  Pallas kernels  151 us (96%)
  local copies, waits for them, and re-layouts  4.74 us (3%)
    pallas_call x1, Pallas kernels, step_stage(): pl.pallas_call(functools.partial(step_kernel, owners, sectors), out_shape...  151 us
    unnamed x2, local copies, waits for them, and re-layouts  3.55 us

profile of v3, /device:TPU:0, one launch (start us, length us, event | category | flops | bytes accessed | tf_op | source)
XLA Modules:
  0.0 157.1 jit_solution(16413280235356614205)
XLA Ops:
  1.3 151.1 %step_stage.1 = (bf16[128,1024]{1,0:T(8,128)(2,1)}, f32[8,128]{1,0:T(8,128)}, f32[128,1024]{1,0:T(8,128)}) custom-call(bf16[128,1024]{1,0:T(8,128)(2,1)} %bitcast.6, f32[128,1024]{1,0:T(8,128)} %bitcast.5, s32[1]{0:T(128)S(6)} %copy.12.dim_ref, s32[1,2]{1,0:T(1,128)} %index_ref.1, f32[16]{0:T(128)} %table_ref.1, bf16[1,2,1024,1024]{3,2,1,0:T(8,128)(2,1)} %left_hbm.1, ...), custom_call_target="tpu_custom_call" | custom-call | flops 21474836480 | bytes 20971520 | tf_op jit(solution)/shard_map/step_stage/pallas_call | solution.py:701
  152.4 1.2 slice.3
  153.6 1.7 %copy.13 = bf16[1,128,1024]{2,1,0:T(8,128)(2,1)} copy(bf16[1,128,1024]{2,1,0:T(8,128)(2,1)} %bitcast.4) | data formatting | bytes 524288
  155.2 1.9 %copy.14 = f32[128,1024]{1,0:T(8,128)} copy(f32[128,1024]{1,0:T(8,128)} %get-tuple-element.14) | data formatting | bytes 1048576

commit v4 on v3

--- a/solution.py
+++ b/solution.py
@@ -20,14 +20,6 @@
 def split2(u):
     high = u.astype(BF16)
     return high, (u - high.astype(F32)).astype(BF16)
-
-
-def split3(u):
-    high = u.astype(BF16).astype(F32)
-    rest = u - high
-    mid = rest.astype(BF16).astype(F32)
-    low = (rest - mid).astype(BF16).astype(F32)
-    return high, mid, low
 
 
 def inverse_factor(block):
@@ -69,12 +61,11 @@
         whole = jnp.concatenate(body, axis=0)
         done.append(whole)
         if at + PANEL < size:
-            high, mid, low = split3(whole)
-            left = jnp.concatenate([high, high, mid, high, mid, low], axis=0)
-            right = jnp.concatenate([high, mid, high, low, mid, high], axis=0)
+            high = whole.astype(BF16).astype(F32)
+            low = whole - high
             outer = jnp.dot(
-                left.T.astype(BF16)[at + PANEL :],
-                right.astype(BF16),
+                jnp.concatenate([high, high, low], axis=0).T.astype(BF16)[at + PANEL :],
+                jnp.concatenate([high, low, high], axis=0).astype(BF16),
                 preferred_element_type=F32,
             )
             lanes = lax.broadcasted_iota(jnp.int32, outer.shape, 1)
@@ -561,9 +552,11 @@
             high, low = split2(jnp.where(col <= row, inverse, 0.0))
             x = columns[...].reshape(order, order)[:, :depth]
             basis[:, lines] = (
-                (
-                    lax.dot_general(x, high, across, preferred_element_type=F32)
-                    + lax.dot_general(x, low, across, preferred_element_type=F32)
+                lax.dot_general(
+                    jnp.concatenate([x, x], axis=1),
+                    jnp.concatenate([high, low], axis=1),
+                    across,
+                    preferred_element_type=F32,
                 )
                 * root
             ).astype(BF16)
@@ -581,16 +574,27 @@
             "sector",
         )
 
-    for p in range(half):
+    width = 2 * rows
+
+    def rotate(p, lines):
         sums[p] = lax.dot_general(
-            basis[:, p * 2 * rows : (p + 1) * 2 * rows],
-            moved[...],
-            (((0,), (0,)), ((), ())),
-            preferred_element_type=F32,
+            lines, moved[...], (((0,), (0,)), ((), ())), preferred_element_type=F32
         ).reshape(2, rows, order) * (1.0 / order)
         given = sums[p, :, pl.ds(pl.multiple_of((1 - core) * part, part), part), :]
         core_out[p] = given.astype(BF16)
         swapping(p).start()
+
+    if width % 128:
+        for p in range(half):
+            rotate(p, basis[:, p * width : (p + 1) * width])
+    else:
+
+        def rotate_in_turn(j, carry):
+            p = turn_of(owners, j)
+            rotate(p, basis[:, pl.ds(pl.multiple_of(p * width, width), width)])
+            return carry
+
+        lax.fori_loop(0, half, rotate_in_turn, 0)
 
     def halves(p):
         swapping(p).wait_recv()
@@ -747,6 +751,33 @@
     )(psi, diag, dim, index, table, left, right)
 
 
+def results_kernel(basis_ref, energy_ref, next_ref, basis_out, energy_out, next_out, sem):
+    copies = [pltpu.make_async_copy(basis_ref, basis_out.at[0], sem.at[0])]
+    copies.append(pltpu.make_async_copy(next_ref, next_out, sem.at[1]))
+    for copy in copies:
+        copy.start()
+    energy_out[0] = jnp.max(energy_ref[...])
+    for copy in copies:
+        copy.wait()
+
+
+def place_results(basis, energy, next_rows):
+    vmem = pl.BlockSpec(memory_space=pltpu.VMEM)
+    hbm = pl.BlockSpec(memory_space=pl.ANY)
+    return pl.pallas_call(
+        results_kernel,
+        out_shape=(
+            jax.ShapeDtypeStruct((1,) + basis.shape, basis.dtype),
+            jax.ShapeDtypeStruct((1,), F32),
+            jax.ShapeDtypeStruct(next_rows.shape, F32),
+        ),
+        in_specs=[vmem, vmem, vmem],
+        out_specs=(hbm, pl.BlockSpec(memory_space=pltpu.SMEM), hbm),
+        scratch_shapes=[pltpu.SemaphoreType.DMA((2,))],
+        name="place_results",
+    )(basis, energy, next_rows)
+
+
 def shards(wavefunction, diag_scale, sector_dims, left_ops, right_ops, weight_index, weight_table):
     basis, energy, next_rows = step_stage(
         wavefunction[0],
@@ -757,7 +788,7 @@
         weight_index,
         weight_table,
     )
-    return (basis[None], energy[0, :1], next_rows)
+    return place_results(basis, energy, next_rows)
 
 
 def solution(mesh):

time: 157 us -> 153 us (0.975)
  local copies, waits for them, and re-layouts: 4.74 us -> 0 us
    unnamed x2 -> x0, local copies, waits for them, and re-layouts: 3.55 us -> none
    pallas_call x0 -> x1, Pallas kernels: none -> 2.54 us  [place_results(): pl.pallas_call(results_kernel, out_shape=(jax.ShapeDtypeStruct((1,) + bas...]
    pallas_call x1, Pallas kernels: 151 us -> 149 us  [step_stage(): pl.pallas_call(functools.partial(step_kernel, owners, sectors), out_shape...]
where the time goes in v4:
time: 153 us
  Pallas kernels  151 us (99%)
    pallas_call x1, Pallas kernels, step_stage(): pl.pallas_call(functools.partial(step_kernel, owners, sectors), out_shape...  149 us

profile of v4, /device:TPU:0, one launch (start us, length us, event | category | flops | bytes accessed | tf_op | source)
XLA Modules:
  0.0 152.6 jit_solution(12716984032281210694)
XLA Ops:
  1.3 148.6 %step_stage.1 = (bf16[128,1024]{1,0:T(8,128)(2,1)}, f32[8,128]{1,0:T(8,128)}, f32[128,1024]{1,0:T(8,128)}) custom-call(bf16[128,1024]{1,0:T(8,128)(2,1)} %bitcast.3, f32[128,1024]{1,0:T(8,128)} %bitcast.2, s32[1]{0:T(128)S(6)} %copy.10.dim_ref, s32[1,2]{1,0:T(1,128)} %index_ref.1, f32[16]{0:T(128)} %table_ref.1, bf16[1,2,1024,1024]{3,2,1,0:T(8,128)(2,1)} %left_hbm.1, ...), custom_call_target="tpu_custom_call" | custom-call | flops 21474836480 | bytes 20971520 | tf_op jit(solution)/shard_map/step_stage/pallas_call | solution.py:705
  149.9 2.5 %place_results.1 = (bf16[1,128,1024]{2,1,0:T(8,128)(2,1)}, f32[1]{0:T(128)}, f32[128,1024]{1,0:T(8,128)}) custom-call(bf16[128,1024]{1,0:T(8,128)(2,1)} %get-tuple-element.6.basis_ref, f32[8,128]{1,0:T(8,128)} %get-tuple-element.7.energy_ref, f32[128,1024]{1,0:T(8,128)} %get-tuple-element.8.next_ref), custom_call_target="tpu_custom_call" | custom-call | tf_op jit(solution)/shard_map/place_results/pallas_call | solution.py:767
